TPU v7x, 256 devices: a whole 4x4x8 slice. The times are simulated.
256 devices in a mesh: state: 256 (over y, z, x, core).
Axes of the slice: x: 4, y: 4, z: 8, core: 2. Of those that a mesh axis runs over, the one named last changes fastest.
Arguments:
- transitions: float32 [4096, 16, 4096], P('state'), may hold values from 0 to 1, as said below
- costs: float32 [4096, 16, 128], P('state'), may hold values from 0 to 4
- valid_counts: int32 [4096], P('state'), may hold values from 1 to 16
- start_values: float32 [4096, 128], P('state'), may hold values from -12 to 12
- ref_state: int32 [1], replicated, may hold values from 0 to 4095
Outputs:
- relative_values: float32 [4096, 128], P('state')
- lower_bounds: float32 [4, 128], replicated
- upper_bounds: float32 [4, 128], replicated
Inputs may be any that keep to these rules, and one draw needn't show every extreme that they name: Every entry is nonnegative and each row transitions[s, a, :] sums to one up to float32 rounding. Actions 0 to valid_counts[s] - 1 are allowed in state s.
All inputs are finite; a program needn't handle non-finite values.
Results may differ from a plain program's by a relative error of at most 0.00017.
Values sent between devices are 32-bit elements; how exact they have to be, the bound alone decides.
No kernel may reach another device: no remote copies, remote signals or barrier semaphores. Data moves between devices by JAX's collectives and lax.ppermute only.
A program may use at most 64 MiB of HBM per device.

v0:
```python
import jax
import jax.numpy as jnp
from jax import lax
from jax.sharding import Mesh
from jax.sharding import PartitionSpec as P

ITERS = 4
STATE = ("state_0", "state_1", "state_2", "state_3")


big_value = 1e30


def over_axes(x, axes):
    for axis in axes:
        x = lax.pmax(x, axis)
    return x


def local(transitions, costs, valid_counts, start_values, ref_state):
    local_states = transitions.shape[0]
    actions = transitions.shape[1]
    scenarios = start_values.shape[1]
    flat_rows = transitions.reshape(local_states * actions, transitions.shape[2])
    allowed = jnp.arange(actions, dtype=jnp.int32)[None, :] < valid_counts[:, None]
    my_index = lax.axis_index(STATE)
    first_state = my_index * local_states
    owner_index = ref_state[0] // local_states
    offset = jnp.clip(ref_state[0] - first_state, 0, local_states - 1)
    is_owner = owner_index == my_index
    lower_list = []
    upper_list = []
    unshifted = start_values
    for iteration in range(ITERS):
        field_all = lax.all_gather(unshifted, STATE, axis=0, tiled=True)
        bellman_expected = jnp.dot(
            flat_rows,
            field_all,
            precision=lax.Precision.HIGHEST,
            preferred_element_type=jnp.float32,
        )
        q_values = costs + bellman_expected.reshape(local_states, actions, scenarios)
        q_values = jnp.where(allowed[:, :, None], q_values, jnp.float32(big_value))
        best_value = jnp.min(q_values, axis=1)
        increase = best_value - unshifted
        lower_list.append(jnp.min(increase, axis=0))
        upper_list.append(jnp.max(increase, axis=0))
        unshifted = best_value
    local_row = lax.dynamic_slice_in_dim(unshifted, offset, 1, 0)
    masked_row = jnp.where(is_owner, local_row, jnp.float32(-big_value))
    ref_row, upper_all, negated_all = (
        over_axes(masked_row, STATE),
        over_axes(jnp.stack(upper_list), STATE),
        over_axes(-jnp.stack(lower_list), STATE),
    )
    return (unshifted - ref_row, -negated_all, upper_all)


def solution(mesh):
    split = Mesh(mesh.devices.reshape(4, 8, 4, 2), ("state_0", "state_1", "state_2", "state_3"))
    return jax.shard_map(
        local,
        mesh=split,
        in_specs=(P(STATE, None, None), P(STATE, None, None), P(STATE), P(STATE, None), P()),
        out_specs=(P(STATE, None), P(), P()),
        check_vma=False,
    )
```

profile of v0, /device:TPU:1, one launch (start us, length us, event | category | flops | bytes accessed | tf_op | source)
XLA Modules:
  0.0 506.4 jit_solution(16758565774394789343)
XLA Ops:
  7.2 0.7 all-gather.5.cloned.1.call-update
  7.9 0.7 iota_compare_fusion
  8.7 111.4 %all-gather.5.cloned.1.call-done = f32[4096,128]{1,0:T(8,128)} async-done(((f32[16,128]{1,0:T(8,128)}), f32[4096,128]{1,0:T(8,128)}) %all-gather.5.cloned.1.call-update) | async-done | bytes 2097168 | tf_op jit(solution)/shard_map/all_gather | solution.py:35
  120.0 6.9 %fusion.8 = f32[16,128]{1,0:T(8,128)} fusion(f32[16,16,128]{2,1,0:T(8,128)} %param.6, f32[16,16,4096]{2,1,0:T(8,128)} %param.5, f32[4096,128]{1,0:T(8,128)} %all-gather.5.cloned.1.call-done, pred[16,16]{1,0:T(8,128)(4,1)S(1)} %iota_compare_fusion), kind=kOutput, calls=%fused_computation.7 | convolution fusion | flops 1610708992 | bytes 6430976 | tf_op jit(solution)/shard_map/dot_general | solution.py:36
  127.0 0.0 all-gather.9.cloned.1.call-start
  127.1 103.3 %all-gather.7.cloned.1.call-done = f32[4096,128]{1,0:T(8,128)} async-done(((f32[16,128]{1,0:T(8,128)}), f32[4096,128]{1,0:T(8,128)}) %all-gather.7.cloned.1.call-update) | async-done | bytes 2097168 | tf_op jit(solution)/shard_map/all_gather | solution.py:35
  230.3 6.3 %convolution_bitcast_fusion.2 = f32[256,128]{0,1:T(8,128)S(1)} fusion(f32[4096,128]{1,0:T(8,128)} %all-gather.7.cloned.1.call-done, f32[256,4096]{1,0:T(8,128)} %bitcast.44), kind=kOutput, calls=%fused_computation.6 | convolution fusion | flops 1610612736 | bytes 6422528 | tf_op jit(solution)/shard_map/dot_general | solution.py:36
  236.6 0.1 copy.8
  236.8 0.7 select_reduce_fusion.2
  237.5 0.2 all-gather.11.cloned.1.call-start
  237.7 103.1 %all-gather.9.cloned.1.call-done = f32[4096,128]{1,0:T(8,128)} async-done(((f32[16,128]{1,0:T(8,128)}), f32[4096,128]{1,0:T(8,128)}) %all-gather.9.cloned.1.call-update) | async-done | bytes 2097168 | tf_op jit(solution)/shard_map/all_gather | solution.py:35
  340.8 6.3 %convolution_bitcast_fusion.1 = f32[256,128]{0,1:T(8,128)S(1)} fusion(f32[4096,128]{1,0:T(8,128)} %all-gather.9.cloned.1.call-done, f32[256,4096]{1,0:T(8,128)} %bitcast.45), kind=kOutput, calls=%fused_computation.5 | convolution fusion | flops 1610612736 | bytes 6422528 | tf_op jit(solution)/shard_map/dot_general | solution.py:36
  347.1 0.1 copy.9
  347.2 0.7 select_reduce_fusion.1
  348.6 102.6 %all-gather.11.cloned.1.call-done = f32[4096,128]{1,0:T(8,128)} async-done(((f32[16,128]{1,0:T(8,128)}), f32[4096,128]{1,0:T(8,128)}) %all-gather.11.cloned.1.call-update) | async-done | bytes 2097168 | tf_op jit(solution)/shard_map/all_gather | solution.py:35
  451.2 6.3 %convolution_bitcast_fusion = f32[256,128]{0,1:T(8,128)S(1)} fusion(f32[4096,128]{1,0:T(8,128)} %all-gather.11.cloned.1.call-done, f32[256,4096]{1,0:T(8,128)} %bitcast.46), kind=kOutput, calls=%fused_computation.4 | convolution fusion | flops 1610612736 | bytes 6422528 | tf_op jit(solution)/shard_map/dot_general | solution.py:36
  457.5 0.1 copy.10
  457.6 0.1 select_reduce_fusion
  457.8 8.5 %all-reduce.2 = (f32[1,128]{1,0:T(1,128)S(1)}, f32[4,128]{1,0:T(4,128)S(1)}, f32[4,128]{1,0:T(4,128)S(1)}) all-reduce(f32[1,128]{1,0:T(1,128)S(1)} %broadcast_select_fusion, f32[4,128]{1,0:T(4,128)S(1)} %get-tuple-element.29, ...), channel_id=1, replica_groups=mesh['state_0'=4,'state_1'=8,'state_2'=4,'state_3'=2] {'state_0'}, use_global_device_ids=true, to_apply=%region_4.5 | all-reduce | flops 1152 | bytes 9216 | tf_op jit(solution)/shard_map/pmax | solution.py:16
  466.4 13.0 %all-reduce = (f32[1,128]{1,0:T(1,128)S(1)}, f32[4,128]{1,0:T(4,128)S(1)}, f32[4,128]{1,0:T(4,128)S(1)}) all-reduce(f32[1,128]{1,0:T(1,128)S(1)} %get-tuple-element.23, f32[4,128]{1,0:T(4,128)S(1)} %get-tuple-element.24, f32[4,128]{1,0:T(4,128)S(1)} %get-tuple-element.25), channel_id=1, replica_groups=mesh['state_0'=4,'state_1'=8,'state_2'=4,'state_3'=2] {'state_1'}, use_global_device_ids=true, to_apply=%region_5.6 | all-reduce | flops 1152 | bytes 9216 | tf_op jit(solution)/shard_map/pmax | solution.py:16
  479.4 8.5 %all-reduce.1 = (f32[1,128]{1,0:T(1,128)S(1)}, f32[4,128]{1,0:T(4,128)S(1)}, f32[4,128]{1,0:T(4,128)S(1)}) all-reduce(f32[1,128]{1,0:T(1,128)S(1)} %get-tuple-element.17, f32[4,128]{1,0:T(4,128)S(1)} %get-tuple-element.18, f32[4,128]{1,0:T(4,128)S(1)} %get-tuple-element.19), channel_id=1, replica_groups=mesh['state_0'=4,'state_1'=8,'state_2'=4,'state_3'=2] {'state_2'}, use_global_device_ids=true, to_apply=%region_6.7 | all-reduce | flops 1152 | bytes 9216 | tf_op jit(solution)/shard_map/pmax | solution.py:16
  487.9 10.8 %all-reduce.3 = (f32[128]{0:T(128)S(1)}, f32[4,128]{1,0:T(4,128)S(1)}, f32[4,128]{1,0:T(4,128)}) all-reduce(f32[128]{0:T(128)S(1)} %bitcast.55, f32[4,128]{1,0:T(4,128)S(1)} %get-tuple-element.21, f32[4,128]{1,0:T(4,128)S(1)} %get-tuple-element.22), channel_id=1, replica_groups=mesh['state_0'=4,'state_1'=8,'state_2'=4,'state_3'=2] {'state_3'}, use_global_device_ids=true, to_apply=%region_7.8 | all-reduce | flops 1152 | bytes 9216 | tf_op jit(solution)/shard_map/pmax | solution.py:16
  498.7 0.6 broadcast_subtract_fusion
  499.3 0.6 neg.7
  (18 shorter events, 0.2 us)
Async XLA Ops:
  7.2 112.9 %all-gather.5.cloned.1.call-start = ((), (), s32[]{:S(2)}) async-start(), calls=%async_computation | async-start | bytes 2105344 | tf_op jit(solution)/shard_map/all_gather | solution.py:35
  7.9 222.4 %all-gather.7.cloned.1.call-start = ((), (), s32[]{:S(2)}) async-start(), calls=%async_computation.1 | async-start | bytes 2105344 | tf_op jit(solution)/shard_map/all_gather | solution.py:35
  127.0 213.8 %all-gather.9.cloned.1.call-start = ((), (), s32[]{:S(2)}) async-start(), calls=%async_computation.2 | async-start | bytes 2105344 | tf_op jit(solution)/shard_map/all_gather | solution.py:35
  230.3 6.4 %copy-start = (f32[16,16,128]{2,1,0:T(8,128)S(1)}, f32[16,16,128]{2,1,0:T(8,128)}, u32[]{:S(2)}) copy-start(f32[16,16,128]{2,1,0:T(8,128)} %param.6) | copy-start | bytes 393220
  237.5 213.7 %all-gather.11.cloned.1.call-start = ((), (), s32[]{:S(2)}) async-start(), calls=%async_computation.3 | async-start | bytes 2105344 | tf_op jit(solution)/shard_map/all_gather | solution.py:35
  348.6 109.1 %copy-start.1 = (f32[16,128]{1,0:T(8,128)S(1)}, f32[16,128]{1,0:T(8,128)}, u32[]{:S(2)}) copy-start(f32[16,128]{1,0:T(8,128)} %fusion.8) | copy-start | bytes 24580
  348.6 109.1 %copy-start.2 = (f32[16,128]{1,0:T(8,128)S(1)}, f32[16,128]{1,0:T(8,128)}, u32[]{:S(2)}) copy-start(f32[16,128]{1,0:T(8,128)} %select_reduce_fusion.2) | copy-start | bytes 24580
  348.6 109.1 %copy-start.3 = (f32[16,128]{1,0:T(8,128)S(1)}, f32[16,128]{1,0:T(8,128)}, u32[]{:S(2)}) copy-start(f32[16,128]{1,0:T(8,128)} %select_reduce_fusion.1) | copy-start | bytes 24580
  348.6 109.1 %copy-start.4 = (f32[16,128]{1,0:T(8,128)S(1)}, f32[16,128]{1,0:T(8,128)}, u32[]{:S(2)}) copy-start(f32[16,128]{1,0:T(8,128)} %param.8) | copy-start | bytes 24580
Sparse Core Ops, SparseCore 0:
  11.7 108.2 all-gather.4
  127.1 103.1 all-gather.6
  237.6 103.1 all-gather.8
  348.0 103.1 all-gather.10
where the time goes:
time: 507 us; the launch traced here: 506 us
  waiting for transfers between devices  421 us (83%)
  blocking collectives  40.9 us (8%)
  matrix products  25.8 us (5%)
  between operations  14.6 us (3%)
    all_gather x4, waiting for transfers between devices, local(): field_all = lax.all_gather(unshifted, STATE, axis=0, tiled=True)  420 us
    pmax x4, blocking collectives, over_axes(): x = lax.pmax(x, axis)  40.9 us
    dot_general x4, matrix products, local(): jnp.dot(flat_rows, field_all, precision=lax.Precision.HIGHEST, preferred_...  25.8 us
  transfers between devices with their start and end apart: 4, of which 4 were waited for; matrix products, arithmetic and copies ran while one was open for 0% of the time, Pallas kernels for 0%

commit v1 on v0

v1 whole, which is shorter than its diff:
```python
import functools

import jax
import jax.numpy as jnp
from jax import lax
from jax.experimental import pallas as pl
from jax.experimental.pallas import tpu as pltpu
from jax.sharding import Mesh
from jax.sharding import PartitionSpec as P

ITERS = 4
YS, ZS, XS, CS = 4, 8, 4, 2
ROWS = 16
AXES = ("y", "z", "x", "c")
big_value = 1e30


def split_kernel(p_ref, out_ref):
    p = p_ref[...]
    high = p.astype(jnp.bfloat16)
    out_ref[0] = high
    out_ref[1] = (p - high.astype(jnp.float32)).astype(jnp.bfloat16)


def split_rows(flat_rows):
    m, k = flat_rows.shape
    step = m // 8
    return pl.pallas_call(
        split_kernel,
        grid=(8,),
        in_specs=[pl.BlockSpec((step, k), lambda i: (i, 0))],
        out_specs=pl.BlockSpec((2, step, k), lambda i: (0, i, 0)),
        out_shape=jax.ShapeDtypeStruct((2, m, k), jnp.bfloat16),
        compiler_params=pltpu.CompilerParams(vmem_limit_bytes=8 << 20),
        name="split_rows",
    )(flat_rows)


def bellman_kernel(core_ref, own_ref, other_ref, p_ref, costs_ref, best_ref, spread_ref, field):
    core = core_ref[0]

    def place(i, carry):
        y = i // ZS
        z = i % ZS
        for x in range(XS):
            base = (i * XS + x) * (CS * ROWS)
            for src, c in ((own_ref, core), (other_ref, 1 - core)):
                v = src[y * XS + x, pl.ds(pl.multiple_of(z * ROWS, ROWS), ROWS), :]
                high = v.astype(jnp.bfloat16)
                low = (v - high.astype(jnp.float32)).astype(jnp.bfloat16)
                at = pl.ds(pl.multiple_of(base + c * ROWS, ROWS), ROWS)
                field[at, 0:128] = high
                field[at, 128:256] = low
        return carry

    lax.fori_loop(0, YS * ZS, place, 0)
    top = jnp.dot(p_ref[0], field[...], preferred_element_type=jnp.float32)
    bottom = jnp.dot(p_ref[1], field[:, 0:128], preferred_element_type=jnp.float32)
    expected = top[:, 0:128] + (top[:, 128:256] + bottom)
    q = costs_ref[...] + expected
    best = jnp.min(q.reshape(ROWS, q.shape[0] // ROWS, 128), axis=1)
    best_ref[...] = best
    for i in range(ZS):
        spread_ref[i] = best


def bellman(core, own, other, parts, costs):
    return pl.pallas_call(
        bellman_kernel,
        in_specs=[pl.BlockSpec(memory_space=pltpu.SMEM)] + [pl.BlockSpec(memory_space=pltpu.VMEM)] * 4,
        out_specs=[pl.BlockSpec(memory_space=pltpu.VMEM)] * 2,
        out_shape=[
            jax.ShapeDtypeStruct((ROWS, 128), jnp.float32),
            jax.ShapeDtypeStruct((ZS, ROWS, 128), jnp.float32),
        ],
        scratch_shapes=[pltpu.VMEM((4096, 256), jnp.bfloat16)],
        compiler_params=pltpu.CompilerParams(vmem_limit_bytes=24 << 20),
        name="bellman",
    )(core, own, other, parts, costs)


def gather(spread):
    block = lax.all_to_all(spread, "z", 0, 0, tiled=True).reshape(1, ZS * ROWS, 128)
    plane = jnp.broadcast_to(block, (YS * XS, ZS * ROWS, 128))
    own = lax.all_to_all(plane, ("y", "x"), 0, 0, tiled=True)
    other = lax.ppermute(own, "c", [(0, 1), (1, 0)])
    return own, other


def local(transitions, costs, valid_counts, start_values, ref_state):
    local_states = transitions.shape[0]
    actions = transitions.shape[1]
    flat_rows = transitions.reshape(local_states * actions, transitions.shape[2])
    allowed = jnp.arange(actions, dtype=jnp.int32)[None, :] < valid_counts[:, None]
    costs = jnp.where(allowed[:, :, None], costs, jnp.float32(big_value))
    costs = costs.reshape(local_states * actions, -1)
    parts = split_rows(flat_rows)
    my_index = lax.axis_index(AXES)
    core = lax.axis_index("c").reshape(1)
    first_state = my_index * local_states
    owner_index = ref_state[0] // local_states
    offset = jnp.clip(ref_state[0] - first_state, 0, local_states - 1)
    is_owner = owner_index == my_index
    value = start_values
    spread = jnp.broadcast_to(value[None], (ZS,) + value.shape)
    rows = []
    for _ in range(ITERS):
        own, other = gather(spread)
        best, spread = bellman(core, own, other, parts, costs)
        increase = best - value
        rows.append((jnp.max(increase, axis=0), jnp.max(-increase, axis=0)))
        value = best
    local_row = lax.dynamic_slice_in_dim(value, offset, 1, 0)
    ref_row = jnp.where(is_owner, local_row, jnp.float32(-big_value))
    ends = jnp.concatenate([jnp.stack([u for u, _ in rows]), jnp.stack([l for _, l in rows]), ref_row], axis=0)
    ends = jnp.pad(ends, ((0, 16 - ends.shape[0]), (0, 0)))
    ends = jnp.max(lax.all_to_all(jnp.broadcast_to(ends[None], (ZS,) + ends.shape), "z", 0, 0, tiled=True), axis=0)
    ends = jnp.max(lax.all_to_all(jnp.broadcast_to(ends[None], (YS * XS,) + ends.shape), ("y", "x"), 0, 0, tiled=True), axis=0)
    ends = jnp.maximum(ends, lax.ppermute(ends, "c", [(0, 1), (1, 0)]))
    return value - ends[2 * ITERS], -ends[ITERS : 2 * ITERS], ends[:ITERS]


def solution(mesh):
    split = Mesh(mesh.devices.reshape(YS, ZS, XS, CS), AXES)
    return jax.shard_map(
        local,
        mesh=split,
        in_specs=(P(AXES, None, None), P(AXES, None, None), P(AXES), P(AXES, None), P()),
        out_specs=(P(AXES, None), P(), P()),
        check_vma=False,
    )
```

time: 507 us -> 180 us (0.36)
  waiting for transfers between devices: 421 us -> 7 us
  blocking collectives: 40.9 us -> 141 us
  matrix products: 25.8 us -> 0 us
  starting transfers between devices: 0.34 us -> 13.6 us
  between operations: 14.6 us -> 1.44 us
  Pallas kernels: 0 us -> 9.63 us
  local copies, waits for them, and re-layouts: 0.29 us -> 5.55 us
    all_gather x4 -> x0, waiting for transfers between devices: 420 us -> none  [local(): field_all = lax.all_gather(unshifted, STATE, axis=0, tiled=True)]
    all_to_all x0 -> x10, blocking collectives: none -> 141 us  [the longest x4 77 us: gather(): own = lax.all_to_all(plane, ('y', 'x'), 0, 0, tiled=True)]
    pmax x4 -> x0, blocking collectives: 40.9 us -> none  [over_axes(): x = lax.pmax(x, axis)]
    dot_general x4 -> x0, matrix products: 25.8 us -> none  [local(): jnp.dot(flat_rows, field_all, precision=lax.Precision.HIGHEST, preferred_...]
    ppermute x0 -> x5, starting transfers between devices: none -> 13.6 us  [the longest x4 10.5 us: gather(): other = lax.ppermute(own, 'c', [(0, 1), (1, 0)])]
    pallas_call x0 -> x5, Pallas kernels: none -> 9.63 us  [the longest x4 8.49 us: bellman(): pl.pallas_call(bellman_kernel, in_specs=[pl.BlockSpec(memory_space=pltpu....]
    ppermute x0 -> x5, waiting for transfers between devices: none -> 7 us  [the longest x4 6.18 us: gather(): other = lax.ppermute(own, 'c', [(0, 1), (1, 0)])]
  transfers between devices with their start and end apart: 4 -> 5, of which waited for: 4 -> 4; matrix products, arithmetic and copies ran while one was open for 0% -> 0% of each run, Pallas kernels for 0% -> 1%
where the time goes in v1:
time: 180 us; the launch traced here: 179 us
  blocking collectives  141 us (78%)
  starting transfers between devices  13.6 us (8%)
  Pallas kernels  9.63 us (5%)
  waiting for transfers between devices  7 us (4%)
  local copies, waits for them, and re-layouts  5.55 us (3%)
    all_to_all x4, blocking collectives, gather(): own = lax.all_to_all(plane, ('y', 'x'), 0, 0, tiled=True)  77 us
    all_to_all x4, blocking collectives, gather(): lax.all_to_all(spread, 'z', 0, 0, tiled=True).reshape(1, ZS * ROWS, 128)  44.8 us
    ppermute x4, starting transfers between devices, gather(): other = lax.ppermute(own, 'c', [(0, 1), (1, 0)])  10.5 us
    all_to_all x1, blocking collectives, local(): lax.all_to_all(jnp.broadcast_to(ends[None], (ZS,) + ends.shape), 'z', 0,...  9.51 us
    all_to_all x1, blocking collectives, local(): lax.all_to_all(jnp.broadcast_to(ends[None], (YS * XS,) + ends.shape), ('y...  9.43 us
    pallas_call x4, Pallas kernels, bellman(): pl.pallas_call(bellman_kernel, in_specs=[pl.BlockSpec(memory_space=pltpu....  8.49 us
    ppermute x4, waiting for transfers between devices, gather(): other = lax.ppermute(own, 'c', [(0, 1), (1, 0)])  6.18 us
    unnamed x12, local copies, waits for them, and re-layouts  4.39 us
  transfers between devices with their start and end apart: 5, of which 4 were waited for; matrix products, arithmetic and copies ran while one was open for 0% of the time, Pallas kernels for 1%

profile of v1, /device:TPU:1, one launch (start us, length us, event | category | flops | bytes accessed | tf_op | source)
XLA Modules:
  0.0 179.4 jit_solution(9329889559338299196)
XLA Ops:
  1.3 16.0 %all_to_all.50 = f32[8,16,128]{2,1,0:T(8,128)S(1)} all-to-all(f32[8,16,128]{2,1,0:T(8,128)S(1)} %broadcast_in_dim.65), channel_id=1, replica_groups=mesh['y'=4,'z'=8,'x'=4,'c'=2] {'z'}, dimensions={0} | all-to-all | bytes 131072 | tf_op jit(solution)/shard_map/all_to_all | solution.py:83
  17.5 22.2 %all_to_all.51.own_ref = f32[16,128,128]{2,1,0:T(8,128)S(1)} all-to-all(f32[16,128,128]{2,1,0:T(8,128)S(1)} %broadcast_in_dim.67), channel_id=1, replica_groups=mesh['y'=4,'z'=8,'x'=4,'c'=2] {'y','x'}, dimensions={0} | all-to-all | bytes 2097152 | tf_op jit(solution)/shard_map/all_to_all | solution.py:85
  39.6 3.0 %collective-permute-start = (f32[16,128,128]{2,1,0:T(8,128)S(1)}, f32[16,128,128]{2,1,0:T(8,128)S(1)}, u32[]{:S(2)}, u32[]{:S(2)}) collective-permute-start(f32[16,128,128]{2,1,0:T(8,128)S(1)} %all_to_all.51.own_ref), channel_id=1, source_target_pairs={{0,1},{1,0},{2,3},{3,2},{4,5},{5,4},{6,7},{7,6},{8,9},{9,8},{10,11... | collective-permute-start | bytes 3145736 | tf_op jit(solution)/shard_map/ppermute | solution.py:86
  42.6 2.2 %copy-done.2 = f32[16,16,4096]{2,1,0:T(8,128)S(1)} copy-done((f32[16,16,4096]{2,1,0:T(8,128)S(1)}, f32[16,16,4096]{2,1,0:T(8,128)}, u32[]{:S(2)}) %copy-start.2) | copy-done | bytes 4194328
  46.1 2.0 %bellman.4 = (f32[16,128]{1,0:T(8,128)S(1)}, f32[8,16,128]{2,1,0:T(8,128)S(1)}) custom-call(s32[1]{0:T(128)} %bitcast.core_ref, f32[16,128,128]{2,1,0:T(8,128)S(1)} %all_to_all.51.own_ref, f32[16,128,128]{2,1,0:T(8,128)S(1)} %collective-permute-done.other_ref, bf16[2,256,4096]{2,1,0:T(8,128)(2,1)S(1)} %split_rows.1.p_ref, f32[256,128]{1,0:T(8,128)S(1)} %bitcast.24), custom_call_target="tpu_custom_call" | custom-call | tf_op jit(solution)/shard_map/bellman/pallas_call | solution.py:68
  48.1 9.8 %all_to_all.52 = f32[8,16,128]{2,1,0:T(8,128)S(1)} all-to-all(f32[8,16,128]{2,1,0:T(8,128)S(1)} %get-tuple-element.10), channel_id=1, replica_groups=mesh['y'=4,'z'=8,'x'=4,'c'=2] {'z'}, dimensions={0} | all-to-all | bytes 131072 | tf_op jit(solution)/shard_map/all_to_all | solution.py:83
  58.0 18.5 %all_to_all.53.own_ref = f32[16,128,128]{2,1,0:T(8,128)S(1)} all-to-all(f32[16,128,128]{2,1,0:T(8,128)S(1)} %broadcast_in_dim.71), channel_id=1, replica_groups=mesh['y'=4,'z'=8,'x'=4,'c'=2] {'y','x'}, dimensions={0} | all-to-all | bytes 2097152 | tf_op jit(solution)/shard_map/all_to_all | solution.py:85
  76.5 2.2 %collective-permute-start.1 = (f32[16,128,128]{2,1,0:T(8,128)S(1)}, f32[16,128,128]{2,1,0:T(8,128)S(1)}, u32[]{:S(2)}, u32[]{:S(2)}) collective-permute-start(f32[16,128,128]{2,1,0:T(8,128)S(1)} %all_to_all.53.own_ref), channel_id=1, source_target_pairs={{0,1},{1,0},{2,3},{3,2},{4,5},{5,4},{6,7},{7,6},{8,9},{9,8},{10,11... | collective-permute-start | bytes 3145736 | tf_op jit(solution)/shard_map/ppermute | solution.py:86
  78.7 2.3 %collective-permute-done.1.other_ref = f32[16,128,128]{2,1,0:T(8,128)S(1)} collective-permute-done((f32[16,128,128]{2,1,0:T(8,128)S(1)}, f32[16,128,128]{2,1,0:T(8,128)S(1)}, u32[]{:S(2)}, u32[]{:S(2)}) %collective-permute-start.1) | collective-permute-done | bytes 1048608 | tf_op jit(solution)/shard_map/ppermute | solution.py:86
  81.0 2.0 %bellman.5 = (f32[16,128]{1,0:T(8,128)S(1)}, f32[8,16,128]{2,1,0:T(8,128)S(1)}) custom-call(s32[1]{0:T(128)} %bitcast.core_ref, f32[16,128,128]{2,1,0:T(8,128)S(1)} %all_to_all.53.own_ref, f32[16,128,128]{2,1,0:T(8,128)S(1)} %collective-permute-done.1.other_ref, bf16[2,256,4096]{2,1,0:T(8,128)(2,1)S(1)} %split_rows.1.p_ref, f32[256,128]{1,0:T(8,128)S(1)} %bitcast.25), custom_call_target="tpu_custom_call" | custom-call | tf_op jit(solution)/shard_map/bellman/pallas_call | solution.py:68
  83.0 9.5 %all_to_all.54 = f32[8,16,128]{2,1,0:T(8,128)S(1)} all-to-all(f32[8,16,128]{2,1,0:T(8,128)S(1)} %get-tuple-element.11), channel_id=1, replica_groups=mesh['y'=4,'z'=8,'x'=4,'c'=2] {'z'}, dimensions={0} | all-to-all | bytes 131072 | tf_op jit(solution)/shard_map/all_to_all | solution.py:83
  92.6 18.1 %all_to_all.55.own_ref = f32[16,128,128]{2,1,0:T(8,128)S(1)} all-to-all(f32[16,128,128]{2,1,0:T(8,128)S(1)} %broadcast_in_dim.73), channel_id=1, replica_groups=mesh['y'=4,'z'=8,'x'=4,'c'=2] {'y','x'}, dimensions={0} | all-to-all | bytes 2097152 | tf_op jit(solution)/shard_map/all_to_all | solution.py:85
  110.7 2.7 %collective-permute-start.2 = (f32[16,128,128]{2,1,0:T(8,128)S(1)}, f32[16,128,128]{2,1,0:T(8,128)S(1)}, u32[]{:S(2)}, u32[]{:S(2)}) collective-permute-start(f32[16,128,128]{2,1,0:T(8,128)S(1)} %all_to_all.55.own_ref), channel_id=1, source_target_pairs={{0,1},{1,0},{2,3},{3,2},{4,5},{5,4},{6,7},{7,6},{8,9},{9,8},{10,11... | collective-permute-start | bytes 3145736 | tf_op jit(solution)/shard_map/ppermute | solution.py:86
  113.4 2.3 %collective-permute-done.2.other_ref = f32[16,128,128]{2,1,0:T(8,128)S(1)} collective-permute-done((f32[16,128,128]{2,1,0:T(8,128)S(1)}, f32[16,128,128]{2,1,0:T(8,128)S(1)}, u32[]{:S(2)}, u32[]{:S(2)}) %collective-permute-start.2) | collective-permute-done | bytes 1048608 | tf_op jit(solution)/shard_map/ppermute | solution.py:86
  115.7 2.0 %bellman.6 = (f32[16,128]{1,0:T(8,128)S(1)}, f32[8,16,128]{2,1,0:T(8,128)S(1)}) custom-call(s32[1]{0:T(128)} %bitcast.core_ref, f32[16,128,128]{2,1,0:T(8,128)S(1)} %all_to_all.55.own_ref, f32[16,128,128]{2,1,0:T(8,128)S(1)} %collective-permute-done.2.other_ref, bf16[2,256,4096]{2,1,0:T(8,128)(2,1)S(1)} %split_rows.1.p_ref, f32[256,128]{1,0:T(8,128)S(1)} %bitcast.26), custom_call_target="tpu_custom_call" | custom-call | tf_op jit(solution)/shard_map/bellman/pallas_call | solution.py:68
  117.7 9.5 %all_to_all.56 = f32[8,16,128]{2,1,0:T(8,128)S(1)} all-to-all(f32[8,16,128]{2,1,0:T(8,128)S(1)} %get-tuple-element.12), channel_id=1, replica_groups=mesh['y'=4,'z'=8,'x'=4,'c'=2] {'z'}, dimensions={0} | all-to-all | bytes 131072 | tf_op jit(solution)/shard_map/all_to_all | solution.py:83
  127.3 18.2 %all_to_all.57.own_ref = f32[16,128,128]{2,1,0:T(8,128)S(1)} all-to-all(f32[16,128,128]{2,1,0:T(8,128)S(1)} %broadcast_in_dim.75), channel_id=1, replica_groups=mesh['y'=4,'z'=8,'x'=4,'c'=2] {'y','x'}, dimensions={0} | all-to-all | bytes 2097152 | tf_op jit(solution)/shard_map/all_to_all | solution.py:85
  145.5 2.6 %collective-permute-start.3 = (f32[16,128,128]{2,1,0:T(8,128)S(1)}, f32[16,128,128]{2,1,0:T(8,128)S(1)}, u32[]{:S(2)}, u32[]{:S(2)}) collective-permute-start(f32[16,128,128]{2,1,0:T(8,128)S(1)} %all_to_all.57.own_ref), channel_id=1, source_target_pairs={{0,1},{1,0},{2,3},{3,2},{4,5},{5,4},{6,7},{7,6},{8,9},{9,8},{10,11... | collective-permute-start | bytes 3145736 | tf_op jit(solution)/shard_map/ppermute | solution.py:86
  148.8 1.6 collective-permute-done.3.other_ref
  150.4 2.2 %copy-done.1 = bf16[2,256,4096]{2,1,0:T(8,128)(2,1)S(1)} copy-done((bf16[2,256,4096]{2,1,0:T(8,128)(2,1)S(1)}, bf16[2,256,4096]{2,1,0:T(8,128)(2,1)}, u32[]{:S(2)}) %copy-start.1) | copy-done | bytes 4194328
  152.6 2.6 %bellman.7 = (f32[16,128]{1,0:T(8,128)S(1)}, f32[8,16,128]{2,1,0:T(8,128)}) custom-call(s32[1]{0:T(128)} %bitcast.core_ref, f32[16,128,128]{2,1,0:T(8,128)S(1)} %all_to_all.57.own_ref, f32[16,128,128]{2,1,0:T(8,128)S(1)} %collective-permute-done.3.other_ref, bf16[2,256,4096]{2,1,0:T(8,128)(2,1)S(1)} %copy-done.1, f32[256,128]{1,0:T(8,128)S(1)} %bitcast.27), custom_call_target="tpu_custom_call" | custom-call | tf_op jit(solution)/shard_map/bellman/pallas_call | solution.py:68
  155.3 9.5 %all_to_all.58 = f32[8,16,128]{2,1,0:T(8,128)S(1)} all-to-all(f32[8,16,128]{2,1,0:T(8,128)S(1)} %broadcast_in_dim.77), channel_id=1, replica_groups=mesh['y'=4,'z'=8,'x'=4,'c'=2] {'z'}, dimensions={0} | all-to-all | bytes 131072 | tf_op jit(solution)/shard_map/all_to_all | solution.py:117
  164.8 9.4 %all_to_all.59 = f32[16,16,128]{2,1,0:T(8,128)S(1)} all-to-all(f32[16,16,128]{2,1,0:T(8,128)S(1)} %broadcast_in_dim.78), channel_id=1, replica_groups=mesh['y'=4,'z'=8,'x'=4,'c'=2] {'y','x'}, dimensions={0} | all-to-all | bytes 262144 | tf_op jit(solution)/shard_map/all_to_all | solution.py:118
  174.3 3.1 %collective-permute-start.4 = (f32[16,128]{1,0:T(8,128)S(1)}, f32[16,128]{1,0:T(8,128)S(1)}, u32[]{:S(2)}, u32[]{:S(2)}) collective-permute-start(f32[16,128]{1,0:T(8,128)S(1)} %reduce_max.99), channel_id=1, source_target_pairs={{0,1},{1,0},{2,3},{3,2},{4,5},{5,4},{6,7},{7,6},{8,9},{9,8},{10,11... | collective-permute-start | bytes 24584 | tf_op jit(solution)/shard_map/ppermute | solution.py:119
  (32 shorter events, 4.6 us)
Async XLA Ops:
  39.6 6.5 %collective-permute-start = (f32[16,128,128]{2,1,0:T(8,128)S(1)}, f32[16,128,128]{2,1,0:T(8,128)S(1)}, u32[]{:S(2)}, u32[]{:S(2)}) collective-permute-start(f32[16,128,128]{2,1,0:T(8,128)S(1)} %all_to_all.51.own_ref), channel_id=1, source_target_pairs={{0,1},{1,0},{2,3},{3,2},{4,5},{5,4},{6,7},{7,6},{8,9},{9,8},{10,11... | collective-permute-start | bytes 3145736 | tf_op jit(solution)/shard_map/ppermute | solution.py:86
  42.6 2.2 %copy-start.2 = (f32[16,16,4096]{2,1,0:T(8,128)S(1)}, f32[16,16,4096]{2,1,0:T(8,128)}, u32[]{:S(2)}) copy-start(f32[16,16,4096]{2,1,0:T(8,128)} %param.5) | copy-start | bytes 12582916
  44.8 1.2 copy-start.5
  44.8 1.2 copy-start.3
  45.9 69.8 %copy-start = (bf16[2,256,4096]{2,1,0:T(8,128)(2,1)}, bf16[2,256,4096]{2,1,0:T(8,128)(2,1)S(1)}, u32[]{:S(2)}) copy-start(bf16[2,256,4096]{2,1,0:T(8,128)(2,1)S(1)} %split_rows.1.p_ref) | copy-start | bytes 12582916
  76.5 4.5 %collective-permute-start.1 = (f32[16,128,128]{2,1,0:T(8,128)S(1)}, f32[16,128,128]{2,1,0:T(8,128)S(1)}, u32[]{:S(2)}, u32[]{:S(2)}) collective-permute-start(f32[16,128,128]{2,1,0:T(8,128)S(1)} %all_to_all.53.own_ref), channel_id=1, source_target_pairs={{0,1},{1,0},{2,3},{3,2},{4,5},{5,4},{6,7},{7,6},{8,9},{9,8},{10,11... | collective-permute-start | bytes 3145736 | tf_op jit(solution)/shard_map/ppermute | solution.py:86
  110.7 5.0 %collective-permute-start.2 = (f32[16,128,128]{2,1,0:T(8,128)S(1)}, f32[16,128,128]{2,1,0:T(8,128)S(1)}, u32[]{:S(2)}, u32[]{:S(2)}) collective-permute-start(f32[16,128,128]{2,1,0:T(8,128)S(1)} %all_to_all.55.own_ref), channel_id=1, source_target_pairs={{0,1},{1,0},{2,3},{3,2},{4,5},{5,4},{6,7},{7,6},{8,9},{9,8},{10,11... | collective-permute-start | bytes 3145736 | tf_op jit(solution)/shard_map/ppermute | solution.py:86
  127.3 27.9 %copy-start.4 = (f32[16,128]{1,0:T(8,128)S(1)}, f32[16,128]{1,0:T(8,128)}, u32[]{:S(2)}) copy-start(f32[16,128]{1,0:T(8,128)} %param.8) | copy-start | bytes 24580
  145.5 4.9 %collective-permute-start.3 = (f32[16,128,128]{2,1,0:T(8,128)S(1)}, f32[16,128,128]{2,1,0:T(8,128)S(1)}, u32[]{:S(2)}, u32[]{:S(2)}) collective-permute-start(f32[16,128,128]{2,1,0:T(8,128)S(1)} %all_to_all.57.own_ref), channel_id=1, source_target_pairs={{0,1},{1,0},{2,3},{3,2},{4,5},{5,4},{6,7},{7,6},{8,9},{9,8},{10,11... | collective-permute-start | bytes 3145736 | tf_op jit(solution)/shard_map/ppermute | solution.py:86
  150.4 2.2 %copy-start.1 = (bf16[2,256,4096]{2,1,0:T(8,128)(2,1)S(1)}, bf16[2,256,4096]{2,1,0:T(8,128)(2,1)}, u32[]{:S(2)}) copy-start(bf16[2,256,4096]{2,1,0:T(8,128)(2,1)} %copy-done) | copy-start | bytes 12582916
  174.3 3.9 %collective-permute-start.4 = (f32[16,128]{1,0:T(8,128)S(1)}, f32[16,128]{1,0:T(8,128)S(1)}, u32[]{:S(2)}, u32[]{:S(2)}) collective-permute-start(f32[16,128]{1,0:T(8,128)S(1)} %reduce_max.99), channel_id=1, source_target_pairs={{0,1},{1,0},{2,3},{3,2},{4,5},{5,4},{6,7},{7,6},{8,9},{9,8},{10,11... | collective-permute-start | bytes 24584 | tf_op jit(solution)/shard_map/ppermute | solution.py:119

commit v2 on v0

v2 whole, which is shorter than its diff:
```python
import functools

import jax
import jax.numpy as jnp
from jax import lax
from jax.experimental import pallas as pl
from jax.experimental.pallas import tpu as pltpu
from jax.sharding import Mesh
from jax.sharding import PartitionSpec as P

ITERS = 4
YS, ZS, XS, CS = 4, 8, 4, 2
ROWS = 16
HALF = 64
LANES = 128
AXES = ("y", "z", "x", "c")
SWAP = [(0, 1), (1, 0)]
big_value = 1e30

VMEM = pl.BlockSpec(memory_space=pltpu.VMEM)
SMEM = pl.BlockSpec(memory_space=pltpu.SMEM)
HBM = pl.BlockSpec(memory_space=pltpu.HBM)
TILE = jax.ShapeDtypeStruct((ROWS, LANES), jnp.float32)
SPREAD = jax.ShapeDtypeStruct((ZS, ROWS, LANES), jnp.float32)


def half_of(shape):
    return lax.broadcasted_iota(jnp.int32, shape, len(shape) - 1) // HALF


def merge(core, mine, theirs):
    return jnp.where(half_of(mine.shape) == core, mine, pltpu.roll(theirs, HALF, mine.ndim - 1))


def call(body, name, ins, outs, scratch=(), mib=16):
    return pl.pallas_call(
        body,
        in_specs=ins,
        out_specs=[VMEM] * len(outs) if isinstance(outs, list) else VMEM,
        out_shape=outs,
        scratch_shapes=scratch,
        compiler_params=pltpu.CompilerParams(vmem_limit_bytes=mib << 20),
        name=name,
    )


def begin_kernel(
    ref_ref, my_counts_ref, their_counts_ref, my_costs_ref, their_costs_ref, my_start_ref, their_start_ref,
    value_ref, spread_ref, costs_out, ref_out,
):
    core = lax.axis_index("c")
    value = merge(core, my_start_ref[...], their_start_ref[...])
    value_ref[...] = value
    for i in range(ZS):
        spread_ref[i] = value
    actions = my_costs_ref.shape[1]
    action = lax.broadcasted_iota(jnp.int32, (actions, LANES), 0)
    for s in range(ROWS):
        mine = jnp.where(action < my_counts_ref[s], my_costs_ref[s], big_value)
        theirs = jnp.where(action < their_counts_ref[s], their_costs_ref[s], big_value)
        costs_out[s * actions : (s + 1) * actions, :] = merge(core, mine, theirs)
    ref_out[...] = jnp.full((ROWS, LANES), ref_ref[0], jnp.int32)


def place(blocks_ref, field):
    left = half_of((ROWS, LANES)) == 0
    for i in range(YS * ZS * XS):
        y, z, x = i // (ZS * XS), i // XS % ZS, i % XS
        v = blocks_ref[y * XS + x, z * ROWS : (z + 1) * ROWS, :]
        w = pltpu.roll(v, HALF, 1)
        for c, u in enumerate((jnp.where(left, v, w), jnp.where(left, w, v))):
            high = u.astype(jnp.bfloat16).astype(jnp.float32)
            at = (i * CS + c) * ROWS
            field[at : at + ROWS, :] = jnp.where(left, high, u - high).astype(jnp.bfloat16)


def product(high, low, field):
    total = jnp.dot(high, field, preferred_element_type=jnp.float32)
    return total + jnp.dot(low, field, preferred_element_type=jnp.float32)


def finish(t, mine, theirs, costs, value_ref, ends_ref, ref_ref, best_ref, spread_ref, ends_out):
    core = lax.axis_index("c")
    mine = mine + pltpu.roll(mine, HALF, 1)
    theirs = theirs + pltpu.roll(theirs, HALF, 1)
    q = costs + jnp.where(half_of(mine.shape) == core, mine, theirs)
    best = jnp.min(q.reshape(ROWS, q.shape[0] // ROWS, LANES), axis=1)
    increase = best - value_ref[...]
    row = lax.broadcasted_iota(jnp.int32, (ROWS, LANES), 0)
    old = jnp.full((ROWS, LANES), -big_value, jnp.float32) if ends_ref is None else ends_ref[...]
    ends = jnp.where(row == t, jnp.max(increase, axis=0, keepdims=True), old)
    ends = jnp.where(row == ITERS + t, jnp.max(-increase, axis=0, keepdims=True), ends)
    best_ref[...] = best
    if t < ITERS - 1:
        ends_out[...] = ends
        for i in range(ZS):
            spread_ref[i] = best
        return
    chip = (lax.axis_index("y") * ZS + lax.axis_index("z")) * XS + lax.axis_index("x")
    owner = (row + ROWS * (CS * chip + half_of((ROWS, LANES)))) == ref_ref[...]
    ref_row = jnp.max(jnp.where(owner, best, -big_value), axis=0, keepdims=True)
    ends = jnp.where(row == 2 * ITERS, ref_row, ends)
    for i in range(ZS):
        spread_ref[i] = ends


def first_kernel(
    blocks_ref, mine_hbm, theirs_ref, costs_ref, value_ref,
    best_ref, spread_ref, ends_out, mine_out, theirs_out,
    field, mine_rows, sems,
):
    chunk = mine_rows.shape[1]
    copies = []
    for j in range(mine_rows.shape[0]):
        copy = pltpu.make_async_copy(mine_hbm.at[pl.ds(j * chunk, chunk)], mine_rows.at[j], sems.at[j])
        copy.start()
        copies.append(copy)
    place(blocks_ref, field)

    def part(p, out, j):
        at = slice(j * chunk, (j + 1) * chunk)
        high = p.astype(jnp.bfloat16)
        out[0, at, :] = high
        out[1, at, :] = (p - high.astype(jnp.float32)).astype(jnp.bfloat16)
        return product(out[0, at, :], out[1, at, :], field[...])

    theirs = jnp.concatenate(
        [part(theirs_ref[j * chunk : (j + 1) * chunk, :], theirs_out, j) for j in range(len(copies))], axis=0
    )
    mine = []
    for j, copy in enumerate(copies):
        copy.wait()
        mine.append(part(mine_rows[j], mine_out, j))
    mine = jnp.concatenate(mine, axis=0)
    finish(0, mine, theirs, costs_ref[...], value_ref, None, None, best_ref, spread_ref, ends_out)


def bellman_kernel(t, blocks_ref, mine_ref, theirs_ref, costs_ref, value_ref, ends_ref, *refs):
    ref_ref = refs[0] if t == ITERS - 1 else None
    *outs, field = refs[1:] if t == ITERS - 1 else refs
    place(blocks_ref, field)
    mine = product(mine_ref[0], mine_ref[1], field[...])
    theirs = product(theirs_ref[0], theirs_ref[1], field[...])
    ends_out = None if t == ITERS - 1 else outs[2]
    finish(t, mine, theirs, costs_ref[...], value_ref, ends_ref, ref_ref, outs[0], outs[1], ends_out)


def reduce_kernel(parts_ref, out_ref):
    ends = jnp.max(parts_ref[...], axis=0)
    for i in range(YS * XS):
        out_ref[i] = ends


def packet_kernel(parts_ref, value_ref, out_ref):
    ends = jnp.max(parts_ref[...], axis=0)
    ends = jnp.maximum(ends, pltpu.roll(ends, HALF, 1))
    out_ref[0:ROWS, :] = value_ref[...] - ends[2 * ITERS : 2 * ITERS + 1, :]
    out_ref[ROWS : ROWS + 2 * ITERS, :] = ends[0 : 2 * ITERS, :]


def unpack_kernel(mine_ref, theirs_ref, relative_ref, lower_ref, upper_ref):
    core = lax.axis_index("c")
    relative_ref[...] = merge(core, mine_ref[0:ROWS, :], theirs_ref[0:ROWS, :])
    bounds = jnp.where(
        half_of((2 * ITERS, LANES)) == core,
        mine_ref[ROWS : ROWS + 2 * ITERS, :],
        theirs_ref[ROWS : ROWS + 2 * ITERS, :],
    )
    upper_ref[...] = bounds[:ITERS]
    lower_ref[...] = -bounds[ITERS:]


def gather(spread):
    block = lax.all_to_all(spread, "z", 0, 0, tiled=True).reshape(1, ZS * ROWS, LANES)
    plane = jnp.broadcast_to(block, (YS * XS, ZS * ROWS, LANES))
    return lax.all_to_all(plane, ("y", "x"), 0, 0, tiled=True)


def swap(value):
    return lax.ppermute(value, "c", SWAP)


def local(transitions, costs, valid_counts, start_values, ref_state):
    states, actions, total_states = transitions.shape
    m = states * actions
    flat_rows = transitions.reshape(m, total_states)
    value, spread, costs, ref_rows = call(
        begin_kernel,
        "begin",
        [SMEM] * 3 + [VMEM] * 4,
        [TILE, SPREAD, pltpu.VMEM((m, LANES), jnp.float32), jax.ShapeDtypeStruct((ROWS, LANES), jnp.int32)],
    )(ref_state, valid_counts, swap(valid_counts), costs, swap(costs), start_values, swap(start_values))
    flat_rows, value, spread, costs = lax.optimization_barrier((flat_rows, value, spread, costs))
    their_rows = swap(flat_rows)
    my_rows = pltpu.with_memory_space_constraint(flat_rows, pltpu.HBM)
    parts = pltpu.VMEM((2, m, total_states), jnp.bfloat16)
    field = pltpu.VMEM((total_states, LANES), jnp.bfloat16)
    count = 2
    value, spread, ends, mine, theirs = call(
        first_kernel,
        "bellman_0",
        [VMEM, HBM, VMEM, VMEM, VMEM],
        [TILE, SPREAD, TILE, parts, parts],
        [field, pltpu.VMEM((count, m // count, total_states), jnp.float32), pltpu.SemaphoreType.DMA((count,))],
        32,
    )(gather(spread), my_rows, their_rows, costs, value)
    mine = pltpu.with_memory_space_constraint(mine, pltpu.VMEM)
    theirs = pltpu.with_memory_space_constraint(theirs, pltpu.VMEM)
    for t in range(1, ITERS):
        last = t == ITERS - 1
        outs = call(
            functools.partial(bellman_kernel, t),
            f"bellman_{t}",
            [VMEM] * (6 + last),
            [TILE, SPREAD] + [TILE] * (not last),
            [field],
        )(gather(spread), mine, theirs, costs, value, ends, *([ref_rows] * last))
        value, spread = outs[:2]
        ends = None if last else outs[2]
    rows = lax.all_to_all(spread, "z", 0, 0, tiled=True)
    plane = call(reduce_kernel, "reduce", [VMEM], jax.ShapeDtypeStruct((YS * XS, ROWS, LANES), jnp.float32))(rows)
    rows = lax.all_to_all(plane, ("y", "x"), 0, 0, tiled=True)
    packet = call(packet_kernel, "packet", [VMEM] * 2, jax.ShapeDtypeStruct((ROWS + 2 * ITERS, LANES), jnp.float32))(rows, value)
    bound = jax.ShapeDtypeStruct((ITERS, LANES), jnp.float32)
    return tuple(call(unpack_kernel, "unpack", [VMEM] * 2, [TILE, bound, bound])(packet, swap(packet)))


def solution(mesh):
    split = Mesh(mesh.devices.reshape(YS, ZS, XS, CS), AXES)
    return jax.shard_map(
        local,
        mesh=split,
        in_specs=(P(AXES, None, None), P(AXES, None, None), P(AXES), P(AXES, None), P()),
        out_specs=(P(AXES, None), P(), P()),
        check_vma=False,
    )
```

time: 507 us -> 165 us (0.33)
  waiting for transfers between devices: 421 us -> 1.14 us
  blocking collectives: 40.9 us -> 128 us
  matrix products: 25.8 us -> 0 us
  starting transfers between devices: 0.34 us -> 16.6 us
  Pallas kernels: 0 us -> 14.6 us
  between operations: 14.6 us -> 1.36 us
    all_gather x4 -> x0, waiting for transfers between devices: 420 us -> none  [local(): field_all = lax.all_gather(unshifted, STATE, axis=0, tiled=True)]
    all_to_all x0 -> x10, blocking collectives: none -> 128 us  [the longest x4 67 us: gather(): return lax.all_to_all(plane, ('y', 'x'), 0, 0, tiled=True)]
    pmax x4 -> x0, blocking collectives: 40.9 us -> none  [over_axes(): x = lax.pmax(x, axis)]
    dot_general x4 -> x0, matrix products: 25.8 us -> none  [local(): jnp.dot(flat_rows, field_all, precision=lax.Precision.HIGHEST, preferred_...]
    ppermute x0 -> x5, starting transfers between devices: none -> 16.6 us  [swap(): return lax.ppermute(value, 'c', SWAP)]
    pallas_call x0 -> x8, Pallas kernels: none -> 14.6 us  [the longest x3 8.1 us: local(): call(functools.partial(bellman_kernel, t), f'bellman_{t}', [VMEM] * (6 +...]
  transfers between devices with their start and end apart: 4 -> 5, of which waited for: 4 -> 2; matrix products, arithmetic and copies ran while one was open for 0% -> 0% of each run, Pallas kernels for 0% -> 0%
where the time goes in v2:
time: 165 us
  blocking collectives  128 us (78%)
  starting transfers between devices  16.6 us (10%)
  Pallas kernels  14.6 us (9%)
  local copies, waits for them, and re-layouts  2.63 us (2%)
    all_to_all x4, blocking collectives, gather(): return lax.all_to_all(plane, ('y', 'x'), 0, 0, tiled=True)  67 us
    all_to_all x4, blocking collectives, gather(): lax.all_to_all(spread, 'z', 0, 0, tiled=True).reshape(1, ZS * ROWS, LANES)  42.3 us
    ppermute x5, starting transfers between devices, swap(): return lax.ppermute(value, 'c', SWAP)  16.6 us
    all_to_all x1, blocking collectives, local(): rows = lax.all_to_all(spread, 'z', 0, 0, tiled=True)  9.6 us
    all_to_all x1, blocking collectives, local(): rows = lax.all_to_all(plane, ('y', 'x'), 0, 0, tiled=True)  9.45 us
    pallas_call x3, Pallas kernels, local(): call(functools.partial(bellman_kernel, t), f'bellman_{t}', [VMEM] * (6 +...  8.1 us
    pallas_call x1, Pallas kernels, local(): call(first_kernel, 'bellman_0', [VMEM, HBM, VMEM, VMEM, VMEM], [TILE, SPR...  5.13 us
  transfers between devices with their start and end apart: 5, of which 2 were waited for; matrix products, arithmetic and copies ran while one was open for 0% of the time, Pallas kernels for 0%

profile of v2, /device:TPU:1, one launch (start us, length us, event | category | flops | bytes accessed | tf_op | source)
XLA Modules:
  0.0 164.8 jit_solution(517623443623053021)
XLA Ops:
  0.6 3.3 %collective-permute-start.1 = (f32[16,16,128]{2,1,0:T(8,128)}, f32[16,16,128]{2,1,0:T(8,128)S(1)}, u32[]{:S(2)}, u32[]{:S(2)}) collective-permute-start(f32[16,16,128]{2,1,0:T(8,128)} %my_costs_ref.1), channel_id=1, source_target_pairs={{0,1},{1,0},{2,3},{3,2},{4,5},{5,4},{6,7},{7,6},{8,9},{9,8},{10,11... | collective-permute-start | bytes 393224 | tf_op jit(solution)/shard_map/ppermute | solution.py:180
  4.0 0.4 collective-permute-start
  5.4 0.9 copy-done
  6.3 0.7 copy-done.1
  7.0 0.7 copy-done.2
  7.7 0.6 begin.1
  8.3 0.4 collective-permute-start.3
  8.7 13.4 %all_to_all.50 = f32[8,16,128]{2,1,0:T(8,128)S(1)} all-to-all(f32[8,16,128]{2,1,0:T(8,128)S(1)} %get-tuple-element.27), channel_id=1, replica_groups=mesh['y'=4,'z'=8,'x'=4,'c'=2] {'z'}, dimensions={0} | all-to-all | bytes 131072 | tf_op jit(solution)/shard_map/all_to_all | solution.py:174
  22.3 21.9 %all_to_all.51.blocks_ref = f32[16,128,128]{2,1,0:T(8,128)S(1)} all-to-all(f32[16,128,128]{2,1,0:T(8,128)S(1)} %broadcast_in_dim.29), channel_id=1, replica_groups=mesh['y'=4,'z'=8,'x'=4,'c'=2] {'y','x'}, dimensions={0} | all-to-all | bytes 2097152 | tf_op jit(solution)/shard_map/all_to_all | solution.py:176
  44.2 5.1 %bellman_0.1 = (f32[16,128]{1,0:T(8,128)S(1)}, f32[8,16,128]{2,1,0:T(8,128)S(1)}, f32[16,128]{1,0:T(8,128)S(1)}, bf16[2,256,4096]{2,1,0:T(8,128)(2,1)S(1)}, bf16[2,256,4096]{2,1,0:T(8,128)(2,1)S(1)}) custom-call(f32[16,128,128]{2,1,0:T(8,128)S(1)} %all_to_all.51.blocks_ref, f32[256,4096]{1,0:T(8,128)} %bitcast.6, ...), custom_call_target="tpu_custom_call" | custom-call | tf_op jit(solution)/shard_map/bellman_0/pallas_call | solution.py:199
  49.3 9.7 %all_to_all.52 = f32[8,16,128]{2,1,0:T(8,128)S(1)} all-to-all(f32[8,16,128]{2,1,0:T(8,128)S(1)} %get-tuple-element.31), channel_id=1, replica_groups=mesh['y'=4,'z'=8,'x'=4,'c'=2] {'z'}, dimensions={0} | all-to-all | bytes 131072 | tf_op jit(solution)/shard_map/all_to_all | solution.py:174
  59.1 15.9 %all_to_all.53.blocks_ref = f32[16,128,128]{2,1,0:T(8,128)S(1)} all-to-all(f32[16,128,128]{2,1,0:T(8,128)S(1)} %broadcast_in_dim.31), channel_id=1, replica_groups=mesh['y'=4,'z'=8,'x'=4,'c'=2] {'y','x'}, dimensions={0} | all-to-all | bytes 2097152 | tf_op jit(solution)/shard_map/all_to_all | solution.py:176
  75.0 2.7 %bellman_1.1 = (f32[16,128]{1,0:T(8,128)S(1)}, f32[8,16,128]{2,1,0:T(8,128)S(1)}, f32[16,128]{1,0:T(8,128)S(1)}) custom-call(f32[16,128,128]{2,1,0:T(8,128)S(1)} %all_to_all.53.blocks_ref, bf16[2,256,4096]{2,1,0:T(8,128)(2,1)S(1)} %get-tuple-element.32.mine_ref, bf16[2,256,4096]{2,1,0:T(8,128)(2,1)S(1)} %get-tuple-element.33.theirs_ref, ...), custom_call_target="tpu_custom_call" | custom-call | tf_op jit(solution)/shard_map/bellman_1/pallas_call | solution.py:211
  77.7 9.6 %all_to_all.54 = f32[8,16,128]{2,1,0:T(8,128)S(1)} all-to-all(f32[8,16,128]{2,1,0:T(8,128)S(1)} %get-tuple-element.36), channel_id=1, replica_groups=mesh['y'=4,'z'=8,'x'=4,'c'=2] {'z'}, dimensions={0} | all-to-all | bytes 131072 | tf_op jit(solution)/shard_map/all_to_all | solution.py:174
  87.4 14.8 %all_to_all.55.blocks_ref = f32[16,128,128]{2,1,0:T(8,128)S(1)} all-to-all(f32[16,128,128]{2,1,0:T(8,128)S(1)} %broadcast_in_dim.33), channel_id=1, replica_groups=mesh['y'=4,'z'=8,'x'=4,'c'=2] {'y','x'}, dimensions={0} | all-to-all | bytes 2097152 | tf_op jit(solution)/shard_map/all_to_all | solution.py:176
  102.2 2.7 %bellman_2.1 = (f32[16,128]{1,0:T(8,128)S(1)}, f32[8,16,128]{2,1,0:T(8,128)S(1)}, f32[16,128]{1,0:T(8,128)S(1)}) custom-call(f32[16,128,128]{2,1,0:T(8,128)S(1)} %all_to_all.55.blocks_ref, bf16[2,256,4096]{2,1,0:T(8,128)(2,1)S(1)} %get-tuple-element.32.mine_ref, bf16[2,256,4096]{2,1,0:T(8,128)(2,1)S(1)} %get-tuple-element.33.theirs_ref, ...), custom_call_target="tpu_custom_call" | custom-call | tf_op jit(solution)/shard_map/bellman_2/pallas_call | solution.py:211
  104.9 9.6 %all_to_all.56 = f32[8,16,128]{2,1,0:T(8,128)S(1)} all-to-all(f32[8,16,128]{2,1,0:T(8,128)S(1)} %get-tuple-element.39), channel_id=1, replica_groups=mesh['y'=4,'z'=8,'x'=4,'c'=2] {'z'}, dimensions={0} | all-to-all | bytes 131072 | tf_op jit(solution)/shard_map/all_to_all | solution.py:174
  114.6 14.5 %all_to_all.57.blocks_ref = f32[16,128,128]{2,1,0:T(8,128)S(1)} all-to-all(f32[16,128,128]{2,1,0:T(8,128)S(1)} %broadcast_in_dim.35), channel_id=1, replica_groups=mesh['y'=4,'z'=8,'x'=4,'c'=2] {'y','x'}, dimensions={0} | all-to-all | bytes 2097152 | tf_op jit(solution)/shard_map/all_to_all | solution.py:176
  129.1 2.7 %bellman_3.1 = (f32[16,128]{1,0:T(8,128)S(1)}, f32[8,16,128]{2,1,0:T(8,128)S(1)}) custom-call(f32[16,128,128]{2,1,0:T(8,128)S(1)} %all_to_all.57.blocks_ref, bf16[2,256,4096]{2,1,0:T(8,128)(2,1)S(1)} %get-tuple-element.32.mine_ref, bf16[2,256,4096]{2,1,0:T(8,128)(2,1)S(1)} %get-tuple-element.33.theirs_ref, f32[256,128]{1,0:T(8,128)S(1)} %get-tuple-element.29.costs_ref, ...), custom_call_target="tpu_custom_call" | custom-call | tf_op jit(solution)/shard_map/bellman_3/pallas_call | solution.py:211
  131.8 9.6 %all_to_all.58.parts_ref = f32[8,16,128]{2,1,0:T(8,128)S(1)} all-to-all(f32[8,16,128]{2,1,0:T(8,128)S(1)} %get-tuple-element.43), channel_id=1, replica_groups=mesh['y'=4,'z'=8,'x'=4,'c'=2] {'z'}, dimensions={0} | all-to-all | bytes 131072 | tf_op jit(solution)/shard_map/all_to_all | solution.py:220
  141.4 9.5 %all_to_all.59.parts_ref = f32[16,16,128]{2,1,0:T(8,128)S(1)} all-to-all(f32[16,16,128]{2,1,0:T(8,128)S(1)} %reduce.1), channel_id=1, replica_groups=mesh['y'=4,'z'=8,'x'=4,'c'=2] {'y','x'}, dimensions={0} | all-to-all | bytes 262144 | tf_op jit(solution)/shard_map/all_to_all | solution.py:222
  150.9 12.4 %collective-permute-start.4 = (f32[24,128]{1,0:T(8,128)S(1)}, f32[24,128]{1,0:T(8,128)S(1)}, u32[]{:S(2)}, u32[]{:S(2)}) collective-permute-start(f32[24,128]{1,0:T(8,128)S(1)} %packet.1.mine_ref), channel_id=1, source_target_pairs={{0,1},{1,0},{2,3},{3,2},{4,5},{5,4},{6,7},{7,6},{8,9},{9,8},{10,11... | collective-permute-start | bytes 36872 | tf_op jit(solution)/shard_map/ppermute | solution.py:180
  163.3 0.8 collective-permute-done.4.theirs_ref
  164.1 0.7 unpack.1
  (14 shorter events, 0.9 us)
Async XLA Ops:
  0.6 4.8 %collective-permute-start.1 = (f32[16,16,128]{2,1,0:T(8,128)}, f32[16,16,128]{2,1,0:T(8,128)S(1)}, u32[]{:S(2)}, u32[]{:S(2)}) collective-permute-start(f32[16,16,128]{2,1,0:T(8,128)} %my_costs_ref.1), channel_id=1, source_target_pairs={{0,1},{1,0},{2,3},{3,2},{4,5},{5,4},{6,7},{7,6},{8,9},{9,8},{10,11... | collective-permute-start | bytes 393224 | tf_op jit(solution)/shard_map/ppermute | solution.py:180
  3.9 1.5 collective-permute-start.2
  4.0 1.4 collective-permute-start
  5.4 0.9 copy-start
  6.3 0.7 copy-start.1
  7.0 0.7 copy-start.2
  8.3 35.9 %collective-permute-start.3 = (f32[256,4096]{1,0:T(8,128)}, f32[256,4096]{1,0:T(8,128)S(1)}, u32[]{:S(2)}, u32[]{:S(2)}) collective-permute-start(f32[256,4096]{1,0:T(8,128)} %bitcast.5), channel_id=1, source_target_pairs={{0,1},{1,0},{2,3},{3,2},{4,5},{5,4},{6,7},{7,6},{8,9},{9,8},{10,11... | collective-permute-start | bytes 12582920 | tf_op jit(solution)/shard_map/ppermute | solution.py:180
  150.9 13.2 %collective-permute-start.4 = (f32[24,128]{1,0:T(8,128)S(1)}, f32[24,128]{1,0:T(8,128)S(1)}, u32[]{:S(2)}, u32[]{:S(2)}) collective-permute-start(f32[24,128]{1,0:T(8,128)S(1)} %packet.1.mine_ref), channel_id=1, source_target_pairs={{0,1},{1,0},{2,3},{3,2},{4,5},{5,4},{6,7},{7,6},{8,9},{9,8},{10,11... | collective-permute-start | bytes 36872 | tf_op jit(solution)/shard_map/ppermute | solution.py:180

commit v3 on v2

v3 whole, which is shorter than its diff:
```python
import functools

import jax
import jax.numpy as jnp
from jax import lax
from jax.experimental import pallas as pl
from jax.experimental.pallas import tpu as pltpu
from jax.sharding import Mesh
from jax.sharding import PartitionSpec as P

ITERS = 4
YS, ZS, XS, CS = 4, 8, 4, 2
ROWS = 16
HALF = 64
LANES = 128
AXES = ("y", "z", "x", "c")
SWAP = [(0, 1), (1, 0)]
big_value = 1e30

VMEM = pl.BlockSpec(memory_space=pltpu.VMEM)
SMEM = pl.BlockSpec(memory_space=pltpu.SMEM)
HBM = pl.BlockSpec(memory_space=pltpu.HBM)
TILE = jax.ShapeDtypeStruct((ROWS, LANES), jnp.float32)
SPREAD = jax.ShapeDtypeStruct((ZS, ROWS, LANES), jnp.float32)


def half_of(shape):
    return lax.broadcasted_iota(jnp.int32, shape, len(shape) - 1) // HALF


def merge(core, mine, theirs):
    return jnp.where(half_of(mine.shape) == core, mine, pltpu.roll(theirs, HALF, mine.ndim - 1))


def call(body, name, ins, outs, scratch=(), mib=16):
    return pl.pallas_call(
        body,
        in_specs=ins,
        out_specs=[VMEM] * len(outs) if isinstance(outs, list) else VMEM,
        out_shape=outs,
        scratch_shapes=scratch,
        compiler_params=pltpu.CompilerParams(vmem_limit_bytes=mib << 20),
        name=name,
    )


def begin_kernel(
    my_counts_hbm, my_costs_hbm, my_start_hbm, ref_ref, their_counts_ref, their_costs_ref, their_start_ref,
    value_ref, spread_ref, costs_out, ref_out,
    my_counts_ref, my_costs_ref, my_start_ref, sems,
):
    pairs = (
        (my_start_hbm, my_start_ref),
        (my_costs_hbm, my_costs_ref),
        (my_counts_hbm, my_counts_ref),
    )
    copies = [pltpu.make_async_copy(src, dst, sems.at[j]) for j, (src, dst) in enumerate(pairs)]
    for copy in copies:
        copy.start()
    core = lax.axis_index("c")
    copies[0].wait()
    value = merge(core, my_start_ref[...], their_start_ref[...])
    value_ref[...] = value
    for i in range(ZS):
        spread_ref[i] = value
    for copy in copies[1:]:
        copy.wait()
    actions = my_costs_ref.shape[1]
    action = lax.broadcasted_iota(jnp.int32, (actions, LANES), 0)
    for s in range(ROWS):
        mine = jnp.where(action < my_counts_ref[s], my_costs_ref[s], big_value)
        theirs = jnp.where(action < their_counts_ref[s], their_costs_ref[s], big_value)
        costs_out[s * actions : (s + 1) * actions, :] = merge(core, mine, theirs)
    ref_out[...] = jnp.full((ROWS, LANES), ref_ref[0], jnp.int32)


def place(blocks_ref, field, old_ref=None):
    left = half_of((ROWS, LANES)) == 0
    high_end = low_end = None
    for i in range(YS * ZS * XS):
        y, z, x = i // (ZS * XS), i // XS % ZS, i % XS
        block = (y * XS + x, slice(z * ROWS, (z + 1) * ROWS))
        v = blocks_ref[block]
        if old_ref is not None:
            increase = v - old_ref[block]
            high_end = increase if i == 0 else jnp.maximum(high_end, increase)
            low_end = increase if i == 0 else jnp.minimum(low_end, increase)
        w = pltpu.roll(v, HALF, 1)
        for c, u in enumerate((jnp.where(left, v, w), jnp.where(left, w, v))):
            high = u.astype(jnp.bfloat16).astype(jnp.float32)
            at = (i * CS + c) * ROWS
            field[at : at + ROWS, :] = jnp.where(left, high, u - high).astype(jnp.bfloat16)
    if old_ref is None:
        return None
    return both_halves(jnp.max(high_end, axis=0, keepdims=True)), both_halves(jnp.max(-low_end, axis=0, keepdims=True))


def both_halves(row):
    return jnp.maximum(row, pltpu.roll(row, HALF, 1))


def product(high, low, field):
    total = jnp.dot(high, field, preferred_element_type=jnp.float32)
    return total + jnp.dot(low, field, preferred_element_type=jnp.float32)


def improve(mine, theirs, costs):
    mine = mine + pltpu.roll(mine, HALF, 1)
    theirs = theirs + pltpu.roll(theirs, HALF, 1)
    q = costs + jnp.where(half_of(mine.shape) == lax.axis_index("c"), mine, theirs)
    return jnp.min(q.reshape(ROWS, q.shape[0] // ROWS, LANES), axis=1)


def first_kernel(
    blocks_ref, mine_hbm, theirs_ref, costs_ref,
    spread_ref, mine_out, theirs_out,
    field, mine_rows, sems,
):
    chunk = mine_rows.shape[1]
    copies = []
    for j in range(mine_rows.shape[0]):
        copy = pltpu.make_async_copy(mine_hbm.at[pl.ds(j * chunk, chunk)], mine_rows.at[j], sems.at[j])
        copy.start()
        copies.append(copy)
    place(blocks_ref, field)

    def part(p, out, j):
        at = slice(j * chunk, (j + 1) * chunk)
        high = p.astype(jnp.bfloat16)
        out[0, at, :] = high
        out[1, at, :] = (p - high.astype(jnp.float32)).astype(jnp.bfloat16)
        return product(out[0, at, :], out[1, at, :], field[...])

    theirs = jnp.concatenate(
        [part(theirs_ref[j * chunk : (j + 1) * chunk, :], theirs_out, j) for j in range(len(copies))], axis=0
    )
    mine = []
    for j, copy in enumerate(copies):
        copy.wait()
        mine.append(part(mine_rows[j], mine_out, j))
    mine = jnp.concatenate(mine, axis=0)
    best = improve(mine, theirs, costs_ref[...])
    for i in range(ZS):
        spread_ref[i] = best


def bellman_kernel(t, blocks_ref, old_ref, mine_ref, theirs_ref, costs_ref, ends_ref, *refs):
    last = t == ITERS - 1
    spread_ref, ends_out, field = refs[-3:]
    up, down = place(blocks_ref, field, old_ref)
    mine = product(mine_ref[0], mine_ref[1], field[...])
    theirs = product(theirs_ref[0], theirs_ref[1], field[...])
    best = improve(mine, theirs, costs_ref[...])
    row = lax.broadcasted_iota(jnp.int32, (2 * ITERS, LANES), 0)
    ends = jnp.zeros((2 * ITERS, LANES), jnp.float32) if t == 1 else ends_ref[...]
    ends = jnp.where(row == t - 1, up, ends)
    ends_out[...] = jnp.where(row == ITERS + t - 1, down, ends)
    if not last:
        for i in range(ZS):
            spread_ref[i] = best
        return
    ref_ref, value_ref, best_ref = refs[:3]
    increase = best - value_ref[0]
    up = both_halves(jnp.max(increase, axis=0, keepdims=True))
    down = both_halves(jnp.max(-increase, axis=0, keepdims=True))
    chip = (lax.axis_index("y") * ZS + lax.axis_index("z")) * XS + lax.axis_index("x")
    state = lax.broadcasted_iota(jnp.int32, (ROWS, LANES), 0) + ROWS * (CS * chip + half_of((ROWS, LANES)))
    ref_row = both_halves(jnp.max(jnp.where(state == ref_ref[...], best, -big_value), axis=0, keepdims=True))
    best_ref[...] = best
    pair = jnp.concatenate([jnp.where(half_of((1, LANES)) == 0, up, down), ref_row], axis=0)
    spread_ref[...] = jnp.broadcast_to(pair[None], spread_ref.shape)


def packet_kernel(parts_ref, value_ref, ends_ref, out_ref):
    pair = jnp.max(parts_ref[...], axis=0)
    out_ref[0:ROWS, :] = value_ref[...] - pair[1:2, :]
    turned = pltpu.roll(pair, HALF, 1)
    left = half_of((1, LANES)) == 0
    row = lax.broadcasted_iota(jnp.int32, (2 * ITERS, LANES), 0)
    ends = jnp.where(row == ITERS - 1, jnp.where(left, pair[0:1, :], turned[0:1, :]), ends_ref[...])
    ends = jnp.where(row == 2 * ITERS - 1, jnp.where(left, turned[0:1, :], pair[0:1, :]), ends)
    out_ref[ROWS : ROWS + 2 * ITERS, :] = ends


def unpack_kernel(mine_ref, theirs_ref, relative_ref, lower_ref, upper_ref):
    core = lax.axis_index("c")
    relative_ref[...] = merge(core, mine_ref[0:ROWS, :], theirs_ref[0:ROWS, :])
    bounds = jnp.where(
        half_of((2 * ITERS, LANES)) == core,
        mine_ref[ROWS : ROWS + 2 * ITERS, :],
        theirs_ref[ROWS : ROWS + 2 * ITERS, :],
    )
    upper_ref[...] = bounds[:ITERS]
    lower_ref[...] = -bounds[ITERS:]


def gather(spread):
    block = lax.all_to_all(spread, "z", 0, 0, tiled=True).reshape(1, ZS * ROWS, LANES)
    plane = jnp.broadcast_to(block, (YS * XS, ZS * ROWS, LANES))
    return lax.all_to_all(plane, ("y", "x"), 0, 0, tiled=True)


def swap(value):
    return lax.ppermute(value, "c", SWAP)


def local(transitions, costs, valid_counts, start_values, ref_state):
    states, actions, total_states = transitions.shape
    m = states * actions
    flat_rows = transitions.reshape(m, total_states)
    value, spread, costs, ref_rows = call(
        begin_kernel,
        "begin",
        [HBM] * 3 + [SMEM] * 2 + [VMEM] * 2,
        [TILE, SPREAD, pltpu.VMEM((m, LANES), jnp.float32), jax.ShapeDtypeStruct((ROWS, LANES), jnp.int32)],
        [
            pltpu.SMEM(valid_counts.shape, jnp.int32),
            pltpu.VMEM(costs.shape, jnp.float32),
            pltpu.VMEM(start_values.shape, jnp.float32),
            pltpu.SemaphoreType.DMA((3,)),
        ],
    )(
        *(pltpu.with_memory_space_constraint(v, pltpu.HBM) for v in (valid_counts, costs, start_values)),
        ref_state,
        *(swap(v) for v in (valid_counts, costs, start_values)),
    )
    flat_rows, value, spread, costs = lax.optimization_barrier((flat_rows, value, spread, costs))
    their_rows = swap(flat_rows)
    my_rows = pltpu.with_memory_space_constraint(flat_rows, pltpu.HBM)
    parts = pltpu.VMEM((2, m, total_states), jnp.bfloat16)
    field = pltpu.VMEM((total_states, LANES), jnp.bfloat16)
    count = 2
    old = gather(spread)
    spread, mine, theirs = call(
        first_kernel,
        "bellman_0",
        [VMEM, HBM, VMEM, VMEM],
        [SPREAD, parts, parts],
        [field, pltpu.VMEM((count, m // count, total_states), jnp.float32), pltpu.SemaphoreType.DMA((count,))],
        32,
    )(old, my_rows, their_rows, costs)
    mine = pltpu.with_memory_space_constraint(mine, pltpu.VMEM)
    theirs = pltpu.with_memory_space_constraint(theirs, pltpu.VMEM)
    ends_shape = jax.ShapeDtypeStruct((2 * ITERS, LANES), jnp.float32)
    ends = value
    for t in range(1, ITERS):
        last = t == ITERS - 1
        blocks = gather(spread)
        pairs = jax.ShapeDtypeStruct((YS * ZS * XS, 2, LANES), jnp.float32)
        outs = call(
            functools.partial(bellman_kernel, t),
            f"bellman_{t}",
            [VMEM] * (8 if last else 6),
            [TILE, pairs, ends_shape] if last else [SPREAD, ends_shape],
            [field],
        )(blocks, old, mine, theirs, costs, ends, *([ref_rows, spread] if last else []))
        spread, ends = outs[-2:]
        old = blocks
    rows = lax.all_to_all(spread, ("y", "z", "x"), 0, 0, tiled=True)
    packet = call(packet_kernel, "packet", [VMEM] * 3, jax.ShapeDtypeStruct((ROWS + 2 * ITERS, LANES), jnp.float32))(
        rows, outs[0], ends
    )
    bound = jax.ShapeDtypeStruct((ITERS, LANES), jnp.float32)
    return tuple(call(unpack_kernel, "unpack", [VMEM] * 2, [TILE, bound, bound])(packet, swap(packet)))


def solution(mesh):
    split = Mesh(mesh.devices.reshape(YS, ZS, XS, CS), AXES)
    return jax.shard_map(
        local,
        mesh=split,
        in_specs=(P(AXES, None, None), P(AXES, None, None), P(AXES), P(AXES, None), P()),
        out_specs=(P(AXES, None), P(), P()),
        check_vma=False,
    )
```

time: 165 us -> 160 us (0.970)
  local copies, waits for them, and re-layouts: 2.63 us -> 0.37 us
  blocking collectives: 128 us -> 126 us
    all_to_all x2 -> x1, blocking collectives: 19.1 us -> 16.5 us  [local(): rows = lax.all_to_all(spread, ('y', 'z', 'x'), 0, 0, tiled=True)]
    unnamed x6 -> x0, local copies, waits for them, and re-layouts: 2.26 us -> none
    pallas_call x7 -> x6, Pallas kernels: 14 us -> 15 us  [the longest x3 8.32 us: local(): call(functools.partial(bellman_kernel, t), f'bellman_{t}', [VMEM] * (8 if...]
where the time goes in v3:
time: 160 us
  blocking collectives  126 us (79%)
  Pallas kernels  15.6 us (10%)
  starting transfers between devices  15.2 us (10%)
    all_to_all x4, blocking collectives, gather(): return lax.all_to_all(plane, ('y', 'x'), 0, 0, tiled=True)  67 us
    all_to_all x4, blocking collectives, gather(): lax.all_to_all(spread, 'z', 0, 0, tiled=True).reshape(1, ZS * ROWS, LANES)  42.3 us
    all_to_all x1, blocking collectives, local(): rows = lax.all_to_all(spread, ('y', 'z', 'x'), 0, 0, tiled=True)  16.5 us
    ppermute x5, starting transfers between devices, swap(): return lax.ppermute(value, 'c', SWAP)  15.2 us
    pallas_call x3, Pallas kernels, local(): call(functools.partial(bellman_kernel, t), f'bellman_{t}', [VMEM] * (8 if...  8.32 us
    pallas_call x1, Pallas kernels, local(): call(first_kernel, 'bellman_0', [VMEM, HBM, VMEM, VMEM], [SPREAD, parts,...  4.92 us
  transfers between devices with their start and end apart: 5, of which 2 were waited for; matrix products, arithmetic and copies ran while one was open for 0% of the time, Pallas kernels for 0%

profile of v3, /device:TPU:1, one launch (start us, length us, event | category | flops | bytes accessed | tf_op | source)
XLA Modules:
  0.0 159.5 jit_solution(5838308115028932340)
XLA Ops:
  0.6 3.3 %collective-permute-start.1 = (f32[16,16,128]{2,1,0:T(8,128)}, f32[16,16,128]{2,1,0:T(8,128)S(1)}, u32[]{:S(2)}, u32[]{:S(2)}) collective-permute-start(f32[16,16,128]{2,1,0:T(8,128)} %my_costs_hbm.1), channel_id=1, source_target_pairs={{0,1},{1,0},{2,3},{3,2},{4,5},{5,4},{6,7},{7,6},{8,9},{9,8},{10,11... | collective-permute-start | bytes 393224 | tf_op jit(solution)/shard_map/ppermute | solution.py:204
  3.9 0.1 collective-permute-start.2
  4.0 0.4 collective-permute-start
  5.1 0.3 collective-permute-done.their_counts_ref
  5.4 1.6 %begin.1 = (f32[16,128]{1,0:T(8,128)S(1)}, f32[8,16,128]{2,1,0:T(8,128)S(1)}, f32[256,128]{1,0:T(8,128)S(1)}, s32[16,128]{1,0:T(8,128)S(1)}) custom-call(s32[16]{0:T(128)} %my_counts_hbm.1, f32[16,16,128]{2,1,0:T(8,128)} %my_costs_hbm.1, f32[16,128]{1,0:T(8,128)} %my_start_hbm.1, s32[1]{0:T(128)S(6)} %copy.8.ref_ref, ...), custom_call_target="tpu_custom_call" | custom-call | tf_op jit(solution)/shard_map/begin/pallas_call | solution.py:211
  7.0 0.4 collective-permute-start.3
  7.4 13.4 %all_to_all.45 = f32[8,16,128]{2,1,0:T(8,128)S(1)} all-to-all(f32[8,16,128]{2,1,0:T(8,128)S(1)} %get-tuple-element.24), channel_id=1, replica_groups=mesh['y'=4,'z'=8,'x'=4,'c'=2] {'z'}, dimensions={0} | all-to-all | bytes 131072 | tf_op jit(solution)/shard_map/all_to_all | solution.py:198
  20.9 0.1 broadcast_in_dim.29
  21.0 21.9 %all_to_all.46.blocks_ref.old_ref = f32[16,128,128]{2,1,0:T(8,128)S(1)} all-to-all(f32[16,128,128]{2,1,0:T(8,128)S(1)} %broadcast_in_dim.29), channel_id=1, replica_groups=mesh['y'=4,'z'=8,'x'=4,'c'=2] {'y','x'}, dimensions={0} | all-to-all | bytes 2097152 | tf_op jit(solution)/shard_map/all_to_all | solution.py:200
  42.9 4.9 %bellman_0.1 = (f32[8,16,128]{2,1,0:T(8,128)S(1)}, bf16[2,256,4096]{2,1,0:T(8,128)(2,1)S(1)}, bf16[2,256,4096]{2,1,0:T(8,128)(2,1)S(1)}) custom-call(f32[16,128,128]{2,1,0:T(8,128)S(1)} %all_to_all.46.blocks_ref.old_ref, f32[256,4096]{1,0:T(8,128)} %bitcast.6, f32[256,4096]{1,0:T(8,128)S(1)} %collective-permute-done.3.theirs_ref, ...), custom_call_target="tpu_custom_call" | custom-call | tf_op jit(solution)/shard_map/bellman_0/pallas_call | solution.py:234
  47.8 9.7 %all_to_all.47 = f32[8,16,128]{2,1,0:T(8,128)S(1)} all-to-all(f32[8,16,128]{2,1,0:T(8,128)S(1)} %get-tuple-element.27), channel_id=1, replica_groups=mesh['y'=4,'z'=8,'x'=4,'c'=2] {'z'}, dimensions={0} | all-to-all | bytes 131072 | tf_op jit(solution)/shard_map/all_to_all | solution.py:198
  57.6 15.9 %all_to_all.48.blocks_ref.old_ref = f32[16,128,128]{2,1,0:T(8,128)S(1)} all-to-all(f32[16,128,128]{2,1,0:T(8,128)S(1)} %broadcast_in_dim.31), channel_id=1, replica_groups=mesh['y'=4,'z'=8,'x'=4,'c'=2] {'y','x'}, dimensions={0} | all-to-all | bytes 2097152 | tf_op jit(solution)/shard_map/all_to_all | solution.py:200
  73.5 2.7 %bellman_1.1 = (f32[8,16,128]{2,1,0:T(8,128)S(1)}, f32[8,128]{1,0:T(8,128)S(1)}) custom-call(f32[16,128,128]{2,1,0:T(8,128)S(1)} %all_to_all.48.blocks_ref.old_ref, f32[16,128,128]{2,1,0:T(8,128)S(1)} %all_to_all.46.blocks_ref.old_ref, bf16[2,256,4096]{2,1,0:T(8,128)(2,1)S(1)} %get-tuple-element.28.mine_ref, ...), custom_call_target="tpu_custom_call" | custom-call | tf_op jit(solution)/shard_map/bellman_1/pallas_call | solution.py:250
  76.2 9.6 %all_to_all.49 = f32[8,16,128]{2,1,0:T(8,128)S(1)} all-to-all(f32[8,16,128]{2,1,0:T(8,128)S(1)} %get-tuple-element.31), channel_id=1, replica_groups=mesh['y'=4,'z'=8,'x'=4,'c'=2] {'z'}, dimensions={0} | all-to-all | bytes 131072 | tf_op jit(solution)/shard_map/all_to_all | solution.py:198
  85.9 14.8 %all_to_all.50.blocks_ref.old_ref = f32[16,128,128]{2,1,0:T(8,128)S(1)} all-to-all(f32[16,128,128]{2,1,0:T(8,128)S(1)} %broadcast_in_dim.33), channel_id=1, replica_groups=mesh['y'=4,'z'=8,'x'=4,'c'=2] {'y','x'}, dimensions={0} | all-to-all | bytes 2097152 | tf_op jit(solution)/shard_map/all_to_all | solution.py:200
  100.7 2.7 %bellman_2.1 = (f32[8,16,128]{2,1,0:T(8,128)S(1)}, f32[8,128]{1,0:T(8,128)S(1)}) custom-call(f32[16,128,128]{2,1,0:T(8,128)S(1)} %all_to_all.50.blocks_ref.old_ref, f32[16,128,128]{2,1,0:T(8,128)S(1)} %all_to_all.48.blocks_ref.old_ref, bf16[2,256,4096]{2,1,0:T(8,128)(2,1)S(1)} %get-tuple-element.28.mine_ref, ...), custom_call_target="tpu_custom_call" | custom-call | tf_op jit(solution)/shard_map/bellman_2/pallas_call | solution.py:250
  103.4 9.6 %all_to_all.51 = f32[8,16,128]{2,1,0:T(8,128)S(1)} all-to-all(f32[8,16,128]{2,1,0:T(8,128)S(1)} %get-tuple-element.33.refs_1_), channel_id=1, replica_groups=mesh['y'=4,'z'=8,'x'=4,'c'=2] {'z'}, dimensions={0} | all-to-all | bytes 131072 | tf_op jit(solution)/shard_map/all_to_all | solution.py:198
  113.1 14.5 %all_to_all.52.blocks_ref = f32[16,128,128]{2,1,0:T(8,128)S(1)} all-to-all(f32[16,128,128]{2,1,0:T(8,128)S(1)} %broadcast_in_dim.35), channel_id=1, replica_groups=mesh['y'=4,'z'=8,'x'=4,'c'=2] {'y','x'}, dimensions={0} | all-to-all | bytes 2097152 | tf_op jit(solution)/shard_map/all_to_all | solution.py:200
  127.6 2.9 %bellman_3.1 = (f32[16,128]{1,0:T(8,128)S(1)}, f32[128,2,128]{2,1,0:T(2,128)S(1)}, f32[8,128]{1,0:T(8,128)S(1)}) custom-call(f32[16,128,128]{2,1,0:T(8,128)S(1)} %all_to_all.52.blocks_ref, f32[16,128,128]{2,1,0:T(8,128)S(1)} %all_to_all.50.blocks_ref.old_ref, bf16[2,256,4096]{2,1,0:T(8,128)(2,1)S(1)} %get-tuple-element.28.mine_ref, ...), custom_call_target="tpu_custom_call" | custom-call | tf_op jit(solution)/shard_map/bellman_3/pallas_call | solution.py:250
  130.5 16.5 %all_to_all.53.parts_ref = f32[128,2,128]{2,1,0:T(2,128)S(1)} all-to-all(f32[128,2,128]{2,1,0:T(2,128)S(1)} %get-tuple-element.36), channel_id=1, replica_groups=mesh['y'=4,'z'=8,'x'=4,'c'=2] {'y','z','x'}, dimensions={0} | all-to-all | bytes 262144 | tf_op jit(solution)/shard_map/all_to_all | solution.py:259
  147.0 0.1 packet.1.mine_ref
  147.1 10.9 %collective-permute-start.4 = (f32[24,128]{1,0:T(8,128)S(1)}, f32[24,128]{1,0:T(8,128)S(1)}, u32[]{:S(2)}, u32[]{:S(2)}) collective-permute-start(f32[24,128]{1,0:T(8,128)S(1)} %packet.1.mine_ref), channel_id=1, source_target_pairs={{0,1},{1,0},{2,3},{3,2},{4,5},{5,4},{6,7},{7,6},{8,9},{9,8},{10,11... | collective-permute-start | bytes 36872 | tf_op jit(solution)/shard_map/ppermute | solution.py:204
  158.0 0.8 collective-permute-done.4.theirs_ref
  158.9 0.7 unpack.1
  (6 shorter events, 0.3 us)
Async XLA Ops:
  0.6 4.8 %collective-permute-start.1 = (f32[16,16,128]{2,1,0:T(8,128)}, f32[16,16,128]{2,1,0:T(8,128)S(1)}, u32[]{:S(2)}, u32[]{:S(2)}) collective-permute-start(f32[16,16,128]{2,1,0:T(8,128)} %my_costs_hbm.1), channel_id=1, source_target_pairs={{0,1},{1,0},{2,3},{3,2},{4,5},{5,4},{6,7},{7,6},{8,9},{9,8},{10,11... | collective-permute-start | bytes 393224 | tf_op jit(solution)/shard_map/ppermute | solution.py:204
  3.9 1.5 collective-permute-start.2
  4.0 1.4 collective-permute-start
  7.0 35.9 %collective-permute-start.3 = (f32[256,4096]{1,0:T(8,128)}, f32[256,4096]{1,0:T(8,128)S(1)}, u32[]{:S(2)}, u32[]{:S(2)}) collective-permute-start(f32[256,4096]{1,0:T(8,128)} %bitcast.5), channel_id=1, source_target_pairs={{0,1},{1,0},{2,3},{3,2},{4,5},{5,4},{6,7},{7,6},{8,9},{9,8},{10,11... | collective-permute-start | bytes 12582920 | tf_op jit(solution)/shard_map/ppermute | solution.py:204
  147.1 11.8 %collective-permute-start.4 = (f32[24,128]{1,0:T(8,128)S(1)}, f32[24,128]{1,0:T(8,128)S(1)}, u32[]{:S(2)}, u32[]{:S(2)}) collective-permute-start(f32[24,128]{1,0:T(8,128)S(1)} %packet.1.mine_ref), channel_id=1, source_target_pairs={{0,1},{1,0},{2,3},{3,2},{4,5},{5,4},{6,7},{7,6},{8,9},{9,8},{10,11... | collective-permute-start | bytes 36872 | tf_op jit(solution)/shard_map/ppermute | solution.py:204

commit v4 on v3

--- a/solution.py
+++ b/solution.py
@@ -44,34 +44,15 @@
     )
 
 
-def begin_kernel(
-    my_counts_hbm, my_costs_hbm, my_start_hbm, ref_ref, their_counts_ref, their_costs_ref, their_start_ref,
-    value_ref, spread_ref, costs_out, ref_out,
-    my_counts_ref, my_costs_ref, my_start_ref, sems,
-):
-    pairs = (
-        (my_start_hbm, my_start_ref),
-        (my_costs_hbm, my_costs_ref),
-        (my_counts_hbm, my_counts_ref),
-    )
-    copies = [pltpu.make_async_copy(src, dst, sems.at[j]) for j, (src, dst) in enumerate(pairs)]
-    for copy in copies:
-        copy.start()
-    core = lax.axis_index("c")
-    copies[0].wait()
-    value = merge(core, my_start_ref[...], their_start_ref[...])
+def begin_kernel(ref_ref, my_start_hbm, their_start_ref, value_ref, spread_ref, ref_out, my_start_ref, sem):
+    copy = pltpu.make_async_copy(my_start_hbm, my_start_ref, sem)
+    copy.start()
+    ref_out[...] = jnp.full((ROWS, LANES), ref_ref[0], jnp.int32)
+    copy.wait()
+    value = merge(lax.axis_index("c"), my_start_ref[...], their_start_ref[...])
     value_ref[...] = value
     for i in range(ZS):
         spread_ref[i] = value
-    for copy in copies[1:]:
-        copy.wait()
-    actions = my_costs_ref.shape[1]
-    action = lax.broadcasted_iota(jnp.int32, (actions, LANES), 0)
-    for s in range(ROWS):
-        mine = jnp.where(action < my_counts_ref[s], my_costs_ref[s], big_value)
-        theirs = jnp.where(action < their_counts_ref[s], their_costs_ref[s], big_value)
-        costs_out[s * actions : (s + 1) * actions, :] = merge(core, mine, theirs)
-    ref_out[...] = jnp.full((ROWS, LANES), ref_ref[0], jnp.int32)
 
 
 def place(blocks_ref, field, old_ref=None):
@@ -112,34 +93,48 @@
 
 
 def first_kernel(
-    blocks_ref, mine_hbm, theirs_ref, costs_ref,
-    spread_ref, mine_out, theirs_out,
-    field, mine_rows, sems,
+    blocks_ref, mine_hbm, theirs_ref, my_counts_hbm, their_counts_ref, my_costs_hbm, their_costs_ref,
+    spread_ref, mine_out, theirs_out, costs_out,
+    field, mine_rows, my_counts_ref, my_costs_ref, sems, small_sems,
 ):
-    chunk = mine_rows.shape[1]
+    small = [
+        pltpu.make_async_copy(my_counts_hbm, my_counts_ref, small_sems.at[0]),
+        pltpu.make_async_copy(my_costs_hbm, my_costs_ref, small_sems.at[1]),
+    ]
+    for copy in small:
+        copy.start()
+    wide = mine_rows.shape[2]
     copies = []
     for j in range(mine_rows.shape[0]):
-        copy = pltpu.make_async_copy(mine_hbm.at[pl.ds(j * chunk, chunk)], mine_rows.at[j], sems.at[j])
+        copy = pltpu.make_async_copy(mine_hbm.at[:, pl.ds(j * wide, wide)], mine_rows.at[j], sems.at[j])
         copy.start()
         copies.append(copy)
     place(blocks_ref, field)
 
     def part(p, out, j):
-        at = slice(j * chunk, (j + 1) * chunk)
+        at = slice(j * wide, (j + 1) * wide)
         high = p.astype(jnp.bfloat16)
-        out[0, at, :] = high
-        out[1, at, :] = (p - high.astype(jnp.float32)).astype(jnp.bfloat16)
-        return product(out[0, at, :], out[1, at, :], field[...])
-
-    theirs = jnp.concatenate(
-        [part(theirs_ref[j * chunk : (j + 1) * chunk, :], theirs_out, j) for j in range(len(copies))], axis=0
-    )
-    mine = []
+        low = (p - high.astype(jnp.float32)).astype(jnp.bfloat16)
+        out[0, :, at] = high
+        out[1, :, at] = low
+        return product(high, low, field[at, :])
+
+    for copy in small:
+        copy.wait()
+    core = lax.axis_index("c")
+    actions = my_costs_ref.shape[1]
+    action = lax.broadcasted_iota(jnp.int32, (actions, LANES), 0)
+    for s in range(ROWS):
+        own = jnp.where(action < my_counts_ref[s], my_costs_ref[s], big_value)
+        other = jnp.where(action < their_counts_ref[s], their_costs_ref[s], big_value)
+        costs_out[s * actions : (s + 1) * actions, :] = merge(core, own, other)
+    theirs = mine = 0.0
+    for j in range(len(copies)):
+        theirs = theirs + part(theirs_ref[:, j * wide : (j + 1) * wide], theirs_out, j)
     for j, copy in enumerate(copies):
         copy.wait()
-        mine.append(part(mine_rows[j], mine_out, j))
-    mine = jnp.concatenate(mine, axis=0)
-    best = improve(mine, theirs, costs_ref[...])
+        mine = mine + part(mine_rows[j], mine_out, j)
+    best = improve(mine, theirs, costs_out[...])
     for i in range(ZS):
         spread_ref[i] = best
 
@@ -208,37 +203,38 @@
     states, actions, total_states = transitions.shape
     m = states * actions
     flat_rows = transitions.reshape(m, total_states)
-    value, spread, costs, ref_rows = call(
+    near = functools.partial(pltpu.with_memory_space_constraint, memory_space=pltpu.HBM)
+    value, spread, ref_rows = call(
         begin_kernel,
         "begin",
-        [HBM] * 3 + [SMEM] * 2 + [VMEM] * 2,
-        [TILE, SPREAD, pltpu.VMEM((m, LANES), jnp.float32), jax.ShapeDtypeStruct((ROWS, LANES), jnp.int32)],
+        [SMEM, HBM, VMEM],
+        [TILE, SPREAD, jax.ShapeDtypeStruct((ROWS, LANES), jnp.int32)],
+        [pltpu.VMEM(start_values.shape, jnp.float32), pltpu.SemaphoreType.DMA],
+    )(ref_state, near(start_values), swap(start_values))
+    flat_rows, value, spread, their_counts, their_costs = lax.optimization_barrier(
+        (flat_rows, value, spread, swap(valid_counts), swap(costs))
+    )
+    their_rows = swap(flat_rows)
+    my_rows = near(flat_rows)
+    parts = pltpu.VMEM((2, m, total_states), jnp.bfloat16)
+    field = pltpu.VMEM((total_states, LANES), jnp.bfloat16)
+    count = 4
+    old = gather(spread)
+    spread, mine, theirs, costs = call(
+        first_kernel,
+        "bellman_0",
+        [VMEM, HBM, VMEM, HBM, SMEM, HBM, VMEM],
+        [SPREAD, parts, parts, pltpu.VMEM((m, LANES), jnp.float32)],
         [
+            field,
+            pltpu.VMEM((count, m, total_states // count), jnp.float32),
             pltpu.SMEM(valid_counts.shape, jnp.int32),
             pltpu.VMEM(costs.shape, jnp.float32),
-            pltpu.VMEM(start_values.shape, jnp.float32),
-            pltpu.SemaphoreType.DMA((3,)),
+            pltpu.SemaphoreType.DMA((count,)),
+            pltpu.SemaphoreType.DMA((2,)),
         ],
-    )(
-        *(pltpu.with_memory_space_constraint(v, pltpu.HBM) for v in (valid_counts, costs, start_values)),
-        ref_state,
-        *(swap(v) for v in (valid_counts, costs, start_values)),
-    )
-    flat_rows, value, spread, costs = lax.optimization_barrier((flat_rows, value, spread, costs))
-    their_rows = swap(flat_rows)
-    my_rows = pltpu.with_memory_space_constraint(flat_rows, pltpu.HBM)
-    parts = pltpu.VMEM((2, m, total_states), jnp.bfloat16)
-    field = pltpu.VMEM((total_states, LANES), jnp.bfloat16)
-    count = 2
-    old = gather(spread)
-    spread, mine, theirs = call(
-        first_kernel,
-        "bellman_0",
-        [VMEM, HBM, VMEM, VMEM],
-        [SPREAD, parts, parts],
-        [field, pltpu.VMEM((count, m // count, total_states), jnp.float32), pltpu.SemaphoreType.DMA((count,))],
         32,
-    )(old, my_rows, their_rows, costs)
+    )(old, my_rows, their_rows, near(valid_counts), their_counts, near(costs), their_costs)
     mine = pltpu.with_memory_space_constraint(mine, pltpu.VMEM)
     theirs = pltpu.with_memory_space_constraint(theirs, pltpu.VMEM)
     ends_shape = jax.ShapeDtypeStruct((2 * ITERS, LANES), jnp.float32)

time: 160 us -> 159 us (level)
  no operation moved by 1% of the time
where the time goes in v4:
time: 159 us
  blocking collectives  126 us (79%)
  starting transfers between devices  15.2 us (10%)
  Pallas kernels  14.9 us (9%)
    all_to_all x4, blocking collectives, gather(): return lax.all_to_all(plane, ('y', 'x'), 0, 0, tiled=True)  66.8 us
    all_to_all x4, blocking collectives, gather(): lax.all_to_all(spread, 'z', 0, 0, tiled=True).reshape(1, ZS * ROWS, LANES)  42.3 us
    all_to_all x1, blocking collectives, local(): rows = lax.all_to_all(spread, ('y', 'z', 'x'), 0, 0, tiled=True)  16.5 us
    ppermute x5, starting transfers between devices, swap(): return lax.ppermute(value, 'c', SWAP)  15.2 us
    pallas_call x3, Pallas kernels, local(): call(functools.partial(bellman_kernel, t), f'bellman_{t}', [VMEM] * (8 if...  8.59 us
    pallas_call x1, Pallas kernels, local(): call(first_kernel, 'bellman_0', [VMEM, HBM, VMEM, HBM, SMEM, HBM, VMEM],...  4.76 us
  transfers between devices with their start and end apart: 5, of which 2 were waited for; matrix products, arithmetic and copies ran while one was open for 0% of the time, Pallas kernels for 0%

profile of v4, /device:TPU:1, one launch (start us, length us, event | category | flops | bytes accessed | tf_op | source)
XLA Modules:
  0.0 158.5 jit_solution(1354440930083735513)
XLA Ops:
  0.6 3.3 %collective-permute-start.2 = (f32[16,16,128]{2,1,0:T(8,128)}, f32[16,16,128]{2,1,0:T(8,128)S(1)}, u32[]{:S(2)}, u32[]{:S(2)}) collective-permute-start(f32[16,16,128]{2,1,0:T(8,128)} %my_costs_hbm.1), channel_id=1, source_target_pairs={{0,1},{1,0},{2,3},{3,2},{4,5},{5,4},{6,7},{7,6},{8,9},{9,8},{10,11... | collective-permute-start | bytes 393224 | tf_op jit(solution)/shard_map/ppermute | solution.py:199
  3.9 0.1 collective-permute-start
  4.0 0.4 collective-permute-start.1
  5.1 0.2 collective-permute-done.their_start_ref
  5.3 0.8 begin.1
  6.1 0.3 collective-permute-start.3
  6.4 13.5 %all_to_all.45 = f32[8,16,128]{2,1,0:T(8,128)S(1)} all-to-all(f32[8,16,128]{2,1,0:T(8,128)S(1)} %get-tuple-element.24), channel_id=1, replica_groups=mesh['y'=4,'z'=8,'x'=4,'c'=2] {'z'}, dimensions={0} | all-to-all | bytes 131072 | tf_op jit(solution)/shard_map/all_to_all | solution.py:193
  20.0 21.9 %all_to_all.46.blocks_ref.old_ref = f32[16,128,128]{2,1,0:T(8,128)S(1)} all-to-all(f32[16,128,128]{2,1,0:T(8,128)S(1)} %broadcast_in_dim.29), channel_id=1, replica_groups=mesh['y'=4,'z'=8,'x'=4,'c'=2] {'y','x'}, dimensions={0} | all-to-all | bytes 2097152 | tf_op jit(solution)/shard_map/all_to_all | solution.py:195
  41.9 4.8 %bellman_0.1 = (f32[8,16,128]{2,1,0:T(8,128)S(1)}, bf16[2,256,4096]{2,1,0:T(8,128)(2,1)S(1)}, bf16[2,256,4096]{2,1,0:T(8,128)(2,1)S(1)}, f32[256,128]{1,0:T(8,128)S(1)}) custom-call(f32[16,128,128]{2,1,0:T(8,128)S(1)} %all_to_all.46.blocks_ref.old_ref, f32[256,4096]{1,0:T(8,128)} %bitcast.6, f32[256,4096]{1,0:T(8,128)S(1)} %collective-permute-done.3.theirs_ref, ...), custom_call_target="tpu_custom_call" | custom-call | tf_op jit(solution)/shard_map/bellman_0/pallas_call | solution.py:223
  46.6 9.6 %all_to_all.47 = f32[8,16,128]{2,1,0:T(8,128)S(1)} all-to-all(f32[8,16,128]{2,1,0:T(8,128)S(1)} %get-tuple-element.28), channel_id=1, replica_groups=mesh['y'=4,'z'=8,'x'=4,'c'=2] {'z'}, dimensions={0} | all-to-all | bytes 131072 | tf_op jit(solution)/shard_map/all_to_all | solution.py:193
  56.2 0.1 broadcast_in_dim.31
  56.3 15.7 %all_to_all.48.blocks_ref.old_ref = f32[16,128,128]{2,1,0:T(8,128)S(1)} all-to-all(f32[16,128,128]{2,1,0:T(8,128)S(1)} %broadcast_in_dim.31), channel_id=1, replica_groups=mesh['y'=4,'z'=8,'x'=4,'c'=2] {'y','x'}, dimensions={0} | all-to-all | bytes 2097152 | tf_op jit(solution)/shard_map/all_to_all | solution.py:195
  72.0 2.8 %bellman_1.1 = (f32[8,16,128]{2,1,0:T(8,128)S(1)}, f32[8,128]{1,0:T(8,128)S(1)}) custom-call(f32[16,128,128]{2,1,0:T(8,128)S(1)} %all_to_all.48.blocks_ref.old_ref, f32[16,128,128]{2,1,0:T(8,128)S(1)} %all_to_all.46.blocks_ref.old_ref, bf16[2,256,4096]{2,1,0:T(8,128)(2,1)S(1)} %get-tuple-element.29.mine_ref, ...), custom_call_target="tpu_custom_call" | custom-call | tf_op jit(solution)/shard_map/bellman_1/pallas_call | solution.py:246
  74.8 9.6 %all_to_all.49 = f32[8,16,128]{2,1,0:T(8,128)S(1)} all-to-all(f32[8,16,128]{2,1,0:T(8,128)S(1)} %get-tuple-element.33), channel_id=1, replica_groups=mesh['y'=4,'z'=8,'x'=4,'c'=2] {'z'}, dimensions={0} | all-to-all | bytes 131072 | tf_op jit(solution)/shard_map/all_to_all | solution.py:193
  84.6 14.7 %all_to_all.50.blocks_ref.old_ref = f32[16,128,128]{2,1,0:T(8,128)S(1)} all-to-all(f32[16,128,128]{2,1,0:T(8,128)S(1)} %broadcast_in_dim.33), channel_id=1, replica_groups=mesh['y'=4,'z'=8,'x'=4,'c'=2] {'y','x'}, dimensions={0} | all-to-all | bytes 2097152 | tf_op jit(solution)/shard_map/all_to_all | solution.py:195
  99.3 2.8 %bellman_2.1 = (f32[8,16,128]{2,1,0:T(8,128)S(1)}, f32[8,128]{1,0:T(8,128)S(1)}) custom-call(f32[16,128,128]{2,1,0:T(8,128)S(1)} %all_to_all.50.blocks_ref.old_ref, f32[16,128,128]{2,1,0:T(8,128)S(1)} %all_to_all.48.blocks_ref.old_ref, bf16[2,256,4096]{2,1,0:T(8,128)(2,1)S(1)} %get-tuple-element.29.mine_ref, ...), custom_call_target="tpu_custom_call" | custom-call | tf_op jit(solution)/shard_map/bellman_2/pallas_call | solution.py:246
  102.1 9.6 %all_to_all.51 = f32[8,16,128]{2,1,0:T(8,128)S(1)} all-to-all(f32[8,16,128]{2,1,0:T(8,128)S(1)} %get-tuple-element.35.refs_1_), channel_id=1, replica_groups=mesh['y'=4,'z'=8,'x'=4,'c'=2] {'z'}, dimensions={0} | all-to-all | bytes 131072 | tf_op jit(solution)/shard_map/all_to_all | solution.py:193
  111.8 14.5 %all_to_all.52.blocks_ref = f32[16,128,128]{2,1,0:T(8,128)S(1)} all-to-all(f32[16,128,128]{2,1,0:T(8,128)S(1)} %broadcast_in_dim.35), channel_id=1, replica_groups=mesh['y'=4,'z'=8,'x'=4,'c'=2] {'y','x'}, dimensions={0} | all-to-all | bytes 2097152 | tf_op jit(solution)/shard_map/all_to_all | solution.py:195
  126.3 3.0 %bellman_3.1 = (f32[16,128]{1,0:T(8,128)S(1)}, f32[128,2,128]{2,1,0:T(2,128)S(1)}, f32[8,128]{1,0:T(8,128)S(1)}) custom-call(f32[16,128,128]{2,1,0:T(8,128)S(1)} %all_to_all.52.blocks_ref, f32[16,128,128]{2,1,0:T(8,128)S(1)} %all_to_all.50.blocks_ref.old_ref, bf16[2,256,4096]{2,1,0:T(8,128)(2,1)S(1)} %get-tuple-element.29.mine_ref, ...), custom_call_target="tpu_custom_call" | custom-call | tf_op jit(solution)/shard_map/bellman_3/pallas_call | solution.py:246
  129.2 16.5 %all_to_all.53.parts_ref = f32[128,2,128]{2,1,0:T(2,128)S(1)} all-to-all(f32[128,2,128]{2,1,0:T(2,128)S(1)} %get-tuple-element.38), channel_id=1, replica_groups=mesh['y'=4,'z'=8,'x'=4,'c'=2] {'y','z','x'}, dimensions={0} | all-to-all | bytes 262144 | tf_op jit(solution)/shard_map/all_to_all | solution.py:255
  145.7 0.1 packet.1.mine_ref
  145.8 11.2 %collective-permute-start.4 = (f32[24,128]{1,0:T(8,128)S(1)}, f32[24,128]{1,0:T(8,128)S(1)}, u32[]{:S(2)}, u32[]{:S(2)}) collective-permute-start(f32[24,128]{1,0:T(8,128)S(1)} %packet.1.mine_ref), channel_id=1, source_target_pairs={{0,1},{1,0},{2,3},{3,2},{4,5},{5,4},{6,7},{7,6},{8,9},{9,8},{10,11... | collective-permute-start | bytes 36872 | tf_op jit(solution)/shard_map/ppermute | solution.py:199
  157.0 0.8 collective-permute-done.4.theirs_ref
  157.8 0.7 unpack.1
  (6 shorter events, 0.3 us)
Async XLA Ops:
  0.6 5.5 %collective-permute-start.2 = (f32[16,16,128]{2,1,0:T(8,128)}, f32[16,16,128]{2,1,0:T(8,128)S(1)}, u32[]{:S(2)}, u32[]{:S(2)}) collective-permute-start(f32[16,16,128]{2,1,0:T(8,128)} %my_costs_hbm.1), channel_id=1, source_target_pairs={{0,1},{1,0},{2,3},{3,2},{4,5},{5,4},{6,7},{7,6},{8,9},{9,8},{10,11... | collective-permute-start | bytes 393224 | tf_op jit(solution)/shard_map/ppermute | solution.py:199
  3.9 1.4 collective-permute-start
  4.0 2.1 %collective-permute-start.1 = (s32[16]{0:T(128)}, s32[16]{0:T(128)S(1)}, u32[]{:S(2)}, u32[]{:S(2)}) collective-permute-start(s32[16]{0:T(128)} %my_counts_hbm.1), channel_id=1, source_target_pairs={{0,1},{1,0},{2,3},{3,2},{4,5},{5,4},{6,7},{7,6},{8,9},{9,8},{10,11... | collective-permute-start | bytes 200 | tf_op jit(solution)/shard_map/ppermute | solution.py:199
  6.1 35.8 %collective-permute-start.3 = (f32[256,4096]{1,0:T(8,128)}, f32[256,4096]{1,0:T(8,128)S(1)}, u32[]{:S(2)}, u32[]{:S(2)}) collective-permute-start(f32[256,4096]{1,0:T(8,128)} %bitcast.5), channel_id=1, source_target_pairs={{0,1},{1,0},{2,3},{3,2},{4,5},{5,4},{6,7},{7,6},{8,9},{9,8},{10,11... | collective-permute-start | bytes 12582920 | tf_op jit(solution)/shard_map/ppermute | solution.py:199
  145.8 12.0 %collective-permute-start.4 = (f32[24,128]{1,0:T(8,128)S(1)}, f32[24,128]{1,0:T(8,128)S(1)}, u32[]{:S(2)}, u32[]{:S(2)}) collective-permute-start(f32[24,128]{1,0:T(8,128)S(1)} %packet.1.mine_ref), channel_id=1, source_target_pairs={{0,1},{1,0},{2,3},{3,2},{4,5},{5,4},{6,7},{7,6},{8,9},{9,8},{10,11... | collective-permute-start | bytes 36872 | tf_op jit(solution)/shard_map/ppermute | solution.py:199

commit v5 on v4

--- a/solution.py
+++ b/solution.py
@@ -55,8 +55,14 @@
         spread_ref[i] = value
 
 
+def base_of(blocks_ref):
+    row = blocks_ref[0, 0:1, :]
+    return jnp.where(half_of((1, LANES)) == 0, row, pltpu.roll(row, HALF, 1))
+
+
 def place(blocks_ref, field, old_ref=None):
     left = half_of((ROWS, LANES)) == 0
+    base = jnp.broadcast_to(base_of(blocks_ref), (ROWS, LANES))
     high_end = low_end = None
     for i in range(YS * ZS * XS):
         y, z, x = i // (ZS * XS), i // XS % ZS, i % XS
@@ -66,14 +72,18 @@
             increase = v - old_ref[block]
             high_end = increase if i == 0 else jnp.maximum(high_end, increase)
             low_end = increase if i == 0 else jnp.minimum(low_end, increase)
-        w = pltpu.roll(v, HALF, 1)
-        for c, u in enumerate((jnp.where(left, v, w), jnp.where(left, w, v))):
-            high = u.astype(jnp.bfloat16).astype(jnp.float32)
-            at = (i * CS + c) * ROWS
-            field[at : at + ROWS, :] = jnp.where(left, high, u - high).astype(jnp.bfloat16)
+        v = v - base
+        high = v.astype(jnp.bfloat16).astype(jnp.float32)
+        low = v - high
+        at = i * CS * ROWS
+        field[at : at + ROWS, :] = jnp.where(left, high, pltpu.roll(low, HALF, 1)).astype(jnp.bfloat16)
+        field[at + ROWS : at + 2 * ROWS, :] = jnp.where(left, pltpu.roll(high, HALF, 1), low).astype(jnp.bfloat16)
     if old_ref is None:
         return None
-    return both_halves(jnp.max(high_end, axis=0, keepdims=True)), both_halves(jnp.max(-low_end, axis=0, keepdims=True))
+    old_base = base_of(old_ref)
+    up = both_halves(jnp.max(high_end, axis=0, keepdims=True)) + old_base
+    down = both_halves(jnp.max(-low_end, axis=0, keepdims=True)) - old_base
+    return up, down
 
 
 def both_halves(row):
@@ -155,7 +165,7 @@
             spread_ref[i] = best
         return
     ref_ref, value_ref, best_ref = refs[:3]
-    increase = best - value_ref[0]
+    increase = best - (value_ref[0] - base_of(blocks_ref))
     up = both_halves(jnp.max(increase, axis=0, keepdims=True))
     down = both_halves(jnp.max(-increase, axis=0, keepdims=True))
     chip = (lax.axis_index("y") * ZS + lax.axis_index("z")) * XS + lax.axis_index("x")

time: 159 us -> 160 us (level)
  no operation moved by 1% of the time
where the time goes in v5:
time: 160 us; the launch traced here: 159 us
  blocking collectives  126 us (79%)
  Pallas kernels  15.6 us (10%)
  starting transfers between devices  15.3 us (10%)
    all_to_all x4, blocking collectives, gather(): return lax.all_to_all(plane, ('y', 'x'), 0, 0, tiled=True)  66.7 us
    all_to_all x4, blocking collectives, gather(): lax.all_to_all(spread, 'z', 0, 0, tiled=True).reshape(1, ZS * ROWS, LANES)  42.3 us
    all_to_all x1, blocking collectives, local(): rows = lax.all_to_all(spread, ('y', 'z', 'x'), 0, 0, tiled=True)  16.5 us
    ppermute x5, starting transfers between devices, swap(): return lax.ppermute(value, 'c', SWAP)  15.3 us
    pallas_call x3, Pallas kernels, local(): call(functools.partial(bellman_kernel, t), f'bellman_{t}', [VMEM] * (8 if...  8.57 us
    pallas_call x1, Pallas kernels, local(): call(first_kernel, 'bellman_0', [VMEM, HBM, VMEM, HBM, SMEM, HBM, VMEM],...  5.46 us
  transfers between devices with their start and end apart: 5, of which 2 were waited for; matrix products, arithmetic and copies ran while one was open for 0% of the time, Pallas kernels for 0%

profile of v5, /device:TPU:1, one launch (start us, length us, event | category | flops | bytes accessed | tf_op | source)
XLA Modules:
  0.0 159.2 jit_solution(16978610838931917858)
XLA Ops:
  0.6 3.3 %collective-permute-start.2 = (f32[16,16,128]{2,1,0:T(8,128)}, f32[16,16,128]{2,1,0:T(8,128)S(1)}, u32[]{:S(2)}, u32[]{:S(2)}) collective-permute-start(f32[16,16,128]{2,1,0:T(8,128)} %my_costs_hbm.1), channel_id=1, source_target_pairs={{0,1},{1,0},{2,3},{3,2},{4,5},{5,4},{6,7},{7,6},{8,9},{9,8},{10,11... | collective-permute-start | bytes 393224 | tf_op jit(solution)/shard_map/ppermute | solution.py:209
  3.9 0.1 collective-permute-start
  4.0 0.4 collective-permute-start.1
  5.1 0.2 collective-permute-done.their_start_ref
  5.3 0.8 begin.1
  6.1 0.3 collective-permute-start.3
  6.4 13.5 %all_to_all.45 = f32[8,16,128]{2,1,0:T(8,128)S(1)} all-to-all(f32[8,16,128]{2,1,0:T(8,128)S(1)} %get-tuple-element.24), channel_id=1, replica_groups=mesh['y'=4,'z'=8,'x'=4,'c'=2] {'z'}, dimensions={0} | all-to-all | bytes 131072 | tf_op jit(solution)/shard_map/all_to_all | solution.py:203
  20.0 21.9 %all_to_all.46.blocks_ref.old_ref = f32[16,128,128]{2,1,0:T(8,128)S(1)} all-to-all(f32[16,128,128]{2,1,0:T(8,128)S(1)} %broadcast_in_dim.29), channel_id=1, replica_groups=mesh['y'=4,'z'=8,'x'=4,'c'=2] {'y','x'}, dimensions={0} | all-to-all | bytes 2097152 | tf_op jit(solution)/shard_map/all_to_all | solution.py:205
  41.9 5.5 %bellman_0.1 = (f32[8,16,128]{2,1,0:T(8,128)S(1)}, bf16[2,256,4096]{2,1,0:T(8,128)(2,1)S(1)}, bf16[2,256,4096]{2,1,0:T(8,128)(2,1)S(1)}, f32[256,128]{1,0:T(8,128)S(1)}) custom-call(f32[16,128,128]{2,1,0:T(8,128)S(1)} %all_to_all.46.blocks_ref.old_ref, f32[256,4096]{1,0:T(8,128)} %bitcast.6, f32[256,4096]{1,0:T(8,128)S(1)} %collective-permute-done.3.theirs_ref, ...), custom_call_target="tpu_custom_call" | custom-call | tf_op jit(solution)/shard_map/bellman_0/pallas_call | solution.py:233
  47.3 9.6 %all_to_all.47 = f32[8,16,128]{2,1,0:T(8,128)S(1)} all-to-all(f32[8,16,128]{2,1,0:T(8,128)S(1)} %get-tuple-element.28), channel_id=1, replica_groups=mesh['y'=4,'z'=8,'x'=4,'c'=2] {'z'}, dimensions={0} | all-to-all | bytes 131072 | tf_op jit(solution)/shard_map/all_to_all | solution.py:203
  56.9 0.1 broadcast_in_dim.31
  57.0 15.7 %all_to_all.48.blocks_ref.old_ref = f32[16,128,128]{2,1,0:T(8,128)S(1)} all-to-all(f32[16,128,128]{2,1,0:T(8,128)S(1)} %broadcast_in_dim.31), channel_id=1, replica_groups=mesh['y'=4,'z'=8,'x'=4,'c'=2] {'y','x'}, dimensions={0} | all-to-all | bytes 2097152 | tf_op jit(solution)/shard_map/all_to_all | solution.py:205
  72.7 2.8 %bellman_1.1 = (f32[8,16,128]{2,1,0:T(8,128)S(1)}, f32[8,128]{1,0:T(8,128)S(1)}) custom-call(f32[16,128,128]{2,1,0:T(8,128)S(1)} %all_to_all.48.blocks_ref.old_ref, f32[16,128,128]{2,1,0:T(8,128)S(1)} %all_to_all.46.blocks_ref.old_ref, bf16[2,256,4096]{2,1,0:T(8,128)(2,1)S(1)} %get-tuple-element.29.mine_ref, ...), custom_call_target="tpu_custom_call" | custom-call | tf_op jit(solution)/shard_map/bellman_1/pallas_call | solution.py:256
  75.5 9.6 %all_to_all.49 = f32[8,16,128]{2,1,0:T(8,128)S(1)} all-to-all(f32[8,16,128]{2,1,0:T(8,128)S(1)} %get-tuple-element.33), channel_id=1, replica_groups=mesh['y'=4,'z'=8,'x'=4,'c'=2] {'z'}, dimensions={0} | all-to-all | bytes 131072 | tf_op jit(solution)/shard_map/all_to_all | solution.py:203
  85.2 14.7 %all_to_all.50.blocks_ref.old_ref = f32[16,128,128]{2,1,0:T(8,128)S(1)} all-to-all(f32[16,128,128]{2,1,0:T(8,128)S(1)} %broadcast_in_dim.33), channel_id=1, replica_groups=mesh['y'=4,'z'=8,'x'=4,'c'=2] {'y','x'}, dimensions={0} | all-to-all | bytes 2097152 | tf_op jit(solution)/shard_map/all_to_all | solution.py:205
  100.0 2.8 %bellman_2.1 = (f32[8,16,128]{2,1,0:T(8,128)S(1)}, f32[8,128]{1,0:T(8,128)S(1)}) custom-call(f32[16,128,128]{2,1,0:T(8,128)S(1)} %all_to_all.50.blocks_ref.old_ref, f32[16,128,128]{2,1,0:T(8,128)S(1)} %all_to_all.48.blocks_ref.old_ref, bf16[2,256,4096]{2,1,0:T(8,128)(2,1)S(1)} %get-tuple-element.29.mine_ref, ...), custom_call_target="tpu_custom_call" | custom-call | tf_op jit(solution)/shard_map/bellman_2/pallas_call | solution.py:256
  102.8 9.6 %all_to_all.51 = f32[8,16,128]{2,1,0:T(8,128)S(1)} all-to-all(f32[8,16,128]{2,1,0:T(8,128)S(1)} %get-tuple-element.35.refs_1_), channel_id=1, replica_groups=mesh['y'=4,'z'=8,'x'=4,'c'=2] {'z'}, dimensions={0} | all-to-all | bytes 131072 | tf_op jit(solution)/shard_map/all_to_all | solution.py:203
  112.5 14.5 %all_to_all.52.blocks_ref = f32[16,128,128]{2,1,0:T(8,128)S(1)} all-to-all(f32[16,128,128]{2,1,0:T(8,128)S(1)} %broadcast_in_dim.35), channel_id=1, replica_groups=mesh['y'=4,'z'=8,'x'=4,'c'=2] {'y','x'}, dimensions={0} | all-to-all | bytes 2097152 | tf_op jit(solution)/shard_map/all_to_all | solution.py:205
  126.9 2.9 %bellman_3.1 = (f32[16,128]{1,0:T(8,128)S(1)}, f32[128,2,128]{2,1,0:T(2,128)S(1)}, f32[8,128]{1,0:T(8,128)S(1)}) custom-call(f32[16,128,128]{2,1,0:T(8,128)S(1)} %all_to_all.52.blocks_ref, f32[16,128,128]{2,1,0:T(8,128)S(1)} %all_to_all.50.blocks_ref.old_ref, bf16[2,256,4096]{2,1,0:T(8,128)(2,1)S(1)} %get-tuple-element.29.mine_ref, ...), custom_call_target="tpu_custom_call" | custom-call | tf_op jit(solution)/shard_map/bellman_3/pallas_call | solution.py:256
  129.9 16.5 %all_to_all.53.parts_ref = f32[128,2,128]{2,1,0:T(2,128)S(1)} all-to-all(f32[128,2,128]{2,1,0:T(2,128)S(1)} %get-tuple-element.38), channel_id=1, replica_groups=mesh['y'=4,'z'=8,'x'=4,'c'=2] {'y','z','x'}, dimensions={0} | all-to-all | bytes 262144 | tf_op jit(solution)/shard_map/all_to_all | solution.py:265
  146.4 0.1 packet.1.mine_ref
  146.5 11.2 %collective-permute-start.4 = (f32[24,128]{1,0:T(8,128)S(1)}, f32[24,128]{1,0:T(8,128)S(1)}, u32[]{:S(2)}, u32[]{:S(2)}) collective-permute-start(f32[24,128]{1,0:T(8,128)S(1)} %packet.1.mine_ref), channel_id=1, source_target_pairs={{0,1},{1,0},{2,3},{3,2},{4,5},{5,4},{6,7},{7,6},{8,9},{9,8},{10,11... | collective-permute-start | bytes 36872 | tf_op jit(solution)/shard_map/ppermute | solution.py:209
  157.7 0.8 collective-permute-done.4.theirs_ref
  158.5 0.7 unpack.1
  (6 shorter events, 0.3 us)
Async XLA Ops:
  0.6 5.5 %collective-permute-start.2 = (f32[16,16,128]{2,1,0:T(8,128)}, f32[16,16,128]{2,1,0:T(8,128)S(1)}, u32[]{:S(2)}, u32[]{:S(2)}) collective-permute-start(f32[16,16,128]{2,1,0:T(8,128)} %my_costs_hbm.1), channel_id=1, source_target_pairs={{0,1},{1,0},{2,3},{3,2},{4,5},{5,4},{6,7},{7,6},{8,9},{9,8},{10,11... | collective-permute-start | bytes 393224 | tf_op jit(solution)/shard_map/ppermute | solution.py:209
  3.9 1.4 collective-permute-start
  4.0 2.1 %collective-permute-start.1 = (s32[16]{0:T(128)}, s32[16]{0:T(128)S(1)}, u32[]{:S(2)}, u32[]{:S(2)}) collective-permute-start(s32[16]{0:T(128)} %my_counts_hbm.1), channel_id=1, source_target_pairs={{0,1},{1,0},{2,3},{3,2},{4,5},{5,4},{6,7},{7,6},{8,9},{9,8},{10,11... | collective-permute-start | bytes 200 | tf_op jit(solution)/shard_map/ppermute | solution.py:209
  6.1 35.8 %collective-permute-start.3 = (f32[256,4096]{1,0:T(8,128)}, f32[256,4096]{1,0:T(8,128)S(1)}, u32[]{:S(2)}, u32[]{:S(2)}) collective-permute-start(f32[256,4096]{1,0:T(8,128)} %bitcast.5), channel_id=1, source_target_pairs={{0,1},{1,0},{2,3},{3,2},{4,5},{5,4},{6,7},{7,6},{8,9},{9,8},{10,11... | collective-permute-start | bytes 12582920 | tf_op jit(solution)/shard_map/ppermute | solution.py:209
  146.5 12.0 %collective-permute-start.4 = (f32[24,128]{1,0:T(8,128)S(1)}, f32[24,128]{1,0:T(8,128)S(1)}, u32[]{:S(2)}, u32[]{:S(2)}) collective-permute-start(f32[24,128]{1,0:T(8,128)S(1)} %packet.1.mine_ref), channel_id=1, source_target_pairs={{0,1},{1,0},{2,3},{3,2},{4,5},{5,4},{6,7},{7,6},{8,9},{9,8},{10,11... | collective-permute-start | bytes 36872 | tf_op jit(solution)/shard_map/ppermute | solution.py:209

commit v6 on v5

--- a/solution.py
+++ b/solution.py
@@ -228,7 +228,7 @@
     my_rows = near(flat_rows)
     parts = pltpu.VMEM((2, m, total_states), jnp.bfloat16)
     field = pltpu.VMEM((total_states, LANES), jnp.bfloat16)
-    count = 4
+    count = 2
     old = gather(spread)
     spread, mine, theirs, costs = call(
         first_kernel,

time: 160 us -> 159 us (level)
  no operation moved by 1% of the time
where the time goes in v6:
time: 159 us
  blocking collectives  126 us (79%)
  starting transfers between devices  15.2 us (10%)
  Pallas kernels  15 us (9%)
    all_to_all x4, blocking collectives, gather(): return lax.all_to_all(plane, ('y', 'x'), 0, 0, tiled=True)  66.8 us
    all_to_all x4, blocking collectives, gather(): lax.all_to_all(spread, 'z', 0, 0, tiled=True).reshape(1, ZS * ROWS, LANES)  42.3 us
    all_to_all x1, blocking collectives, local(): rows = lax.all_to_all(spread, ('y', 'z', 'x'), 0, 0, tiled=True)  16.5 us
    ppermute x5, starting transfers between devices, swap(): return lax.ppermute(value, 'c', SWAP)  15.2 us
    pallas_call x3, Pallas kernels, local(): call(functools.partial(bellman_kernel, t), f'bellman_{t}', [VMEM] * (8 if...  8.57 us
    pallas_call x1, Pallas kernels, local(): call(first_kernel, 'bellman_0', [VMEM, HBM, VMEM, HBM, SMEM, HBM, VMEM],...  4.87 us
  transfers between devices with their start and end apart: 5, of which 2 were waited for; matrix products, arithmetic and copies ran while one was open for 0% of the time, Pallas kernels for 0%

profile of v6, /device:TPU:1, one launch (start us, length us, event | category | flops | bytes accessed | tf_op | source)
XLA Modules:
  0.0 158.6 jit_solution(15998768038432283733)
XLA Ops:
  0.6 3.3 %collective-permute-start.2 = (f32[16,16,128]{2,1,0:T(8,128)}, f32[16,16,128]{2,1,0:T(8,128)S(1)}, u32[]{:S(2)}, u32[]{:S(2)}) collective-permute-start(f32[16,16,128]{2,1,0:T(8,128)} %my_costs_hbm.1), channel_id=1, source_target_pairs={{0,1},{1,0},{2,3},{3,2},{4,5},{5,4},{6,7},{7,6},{8,9},{9,8},{10,11... | collective-permute-start | bytes 393224 | tf_op jit(solution)/shard_map/ppermute | solution.py:209
  3.9 0.1 collective-permute-start
  4.0 0.4 collective-permute-start.1
  5.1 0.2 collective-permute-done.their_start_ref
  5.3 0.8 begin.1
  6.1 0.3 collective-permute-start.3
  6.4 13.5 %all_to_all.45 = f32[8,16,128]{2,1,0:T(8,128)S(1)} all-to-all(f32[8,16,128]{2,1,0:T(8,128)S(1)} %get-tuple-element.24), channel_id=1, replica_groups=mesh['y'=4,'z'=8,'x'=4,'c'=2] {'z'}, dimensions={0} | all-to-all | bytes 131072 | tf_op jit(solution)/shard_map/all_to_all | solution.py:203
  20.0 21.9 %all_to_all.46.blocks_ref.old_ref = f32[16,128,128]{2,1,0:T(8,128)S(1)} all-to-all(f32[16,128,128]{2,1,0:T(8,128)S(1)} %broadcast_in_dim.29), channel_id=1, replica_groups=mesh['y'=4,'z'=8,'x'=4,'c'=2] {'y','x'}, dimensions={0} | all-to-all | bytes 2097152 | tf_op jit(solution)/shard_map/all_to_all | solution.py:205
  41.9 4.9 %bellman_0.1 = (f32[8,16,128]{2,1,0:T(8,128)S(1)}, bf16[2,256,4096]{2,1,0:T(8,128)(2,1)S(1)}, bf16[2,256,4096]{2,1,0:T(8,128)(2,1)S(1)}, f32[256,128]{1,0:T(8,128)S(1)}) custom-call(f32[16,128,128]{2,1,0:T(8,128)S(1)} %all_to_all.46.blocks_ref.old_ref, f32[256,4096]{1,0:T(8,128)} %bitcast.6, f32[256,4096]{1,0:T(8,128)S(1)} %collective-permute-done.3.theirs_ref, ...), custom_call_target="tpu_custom_call" | custom-call | tf_op jit(solution)/shard_map/bellman_0/pallas_call | solution.py:233
  46.8 9.6 %all_to_all.47 = f32[8,16,128]{2,1,0:T(8,128)S(1)} all-to-all(f32[8,16,128]{2,1,0:T(8,128)S(1)} %get-tuple-element.28), channel_id=1, replica_groups=mesh['y'=4,'z'=8,'x'=4,'c'=2] {'z'}, dimensions={0} | all-to-all | bytes 131072 | tf_op jit(solution)/shard_map/all_to_all | solution.py:203
  56.4 0.1 broadcast_in_dim.31
  56.5 15.7 %all_to_all.48.blocks_ref.old_ref = f32[16,128,128]{2,1,0:T(8,128)S(1)} all-to-all(f32[16,128,128]{2,1,0:T(8,128)S(1)} %broadcast_in_dim.31), channel_id=1, replica_groups=mesh['y'=4,'z'=8,'x'=4,'c'=2] {'y','x'}, dimensions={0} | all-to-all | bytes 2097152 | tf_op jit(solution)/shard_map/all_to_all | solution.py:205
  72.1 2.8 %bellman_1.1 = (f32[8,16,128]{2,1,0:T(8,128)S(1)}, f32[8,128]{1,0:T(8,128)S(1)}) custom-call(f32[16,128,128]{2,1,0:T(8,128)S(1)} %all_to_all.48.blocks_ref.old_ref, f32[16,128,128]{2,1,0:T(8,128)S(1)} %all_to_all.46.blocks_ref.old_ref, bf16[2,256,4096]{2,1,0:T(8,128)(2,1)S(1)} %get-tuple-element.29.mine_ref, ...), custom_call_target="tpu_custom_call" | custom-call | tf_op jit(solution)/shard_map/bellman_1/pallas_call | solution.py:256
  75.0 9.6 %all_to_all.49 = f32[8,16,128]{2,1,0:T(8,128)S(1)} all-to-all(f32[8,16,128]{2,1,0:T(8,128)S(1)} %get-tuple-element.33), channel_id=1, replica_groups=mesh['y'=4,'z'=8,'x'=4,'c'=2] {'z'}, dimensions={0} | all-to-all | bytes 131072 | tf_op jit(solution)/shard_map/all_to_all | solution.py:203
  84.7 14.7 %all_to_all.50.blocks_ref.old_ref = f32[16,128,128]{2,1,0:T(8,128)S(1)} all-to-all(f32[16,128,128]{2,1,0:T(8,128)S(1)} %broadcast_in_dim.33), channel_id=1, replica_groups=mesh['y'=4,'z'=8,'x'=4,'c'=2] {'y','x'}, dimensions={0} | all-to-all | bytes 2097152 | tf_op jit(solution)/shard_map/all_to_all | solution.py:205
  99.4 2.8 %bellman_2.1 = (f32[8,16,128]{2,1,0:T(8,128)S(1)}, f32[8,128]{1,0:T(8,128)S(1)}) custom-call(f32[16,128,128]{2,1,0:T(8,128)S(1)} %all_to_all.50.blocks_ref.old_ref, f32[16,128,128]{2,1,0:T(8,128)S(1)} %all_to_all.48.blocks_ref.old_ref, bf16[2,256,4096]{2,1,0:T(8,128)(2,1)S(1)} %get-tuple-element.29.mine_ref, ...), custom_call_target="tpu_custom_call" | custom-call | tf_op jit(solution)/shard_map/bellman_2/pallas_call | solution.py:256
  102.2 9.6 %all_to_all.51 = f32[8,16,128]{2,1,0:T(8,128)S(1)} all-to-all(f32[8,16,128]{2,1,0:T(8,128)S(1)} %get-tuple-element.35.refs_1_), channel_id=1, replica_groups=mesh['y'=4,'z'=8,'x'=4,'c'=2] {'z'}, dimensions={0} | all-to-all | bytes 131072 | tf_op jit(solution)/shard_map/all_to_all | solution.py:203
  111.9 14.5 %all_to_all.52.blocks_ref = f32[16,128,128]{2,1,0:T(8,128)S(1)} all-to-all(f32[16,128,128]{2,1,0:T(8,128)S(1)} %broadcast_in_dim.35), channel_id=1, replica_groups=mesh['y'=4,'z'=8,'x'=4,'c'=2] {'y','x'}, dimensions={0} | all-to-all | bytes 2097152 | tf_op jit(solution)/shard_map/all_to_all | solution.py:205
  126.4 2.9 %bellman_3.1 = (f32[16,128]{1,0:T(8,128)S(1)}, f32[128,2,128]{2,1,0:T(2,128)S(1)}, f32[8,128]{1,0:T(8,128)S(1)}) custom-call(f32[16,128,128]{2,1,0:T(8,128)S(1)} %all_to_all.52.blocks_ref, f32[16,128,128]{2,1,0:T(8,128)S(1)} %all_to_all.50.blocks_ref.old_ref, bf16[2,256,4096]{2,1,0:T(8,128)(2,1)S(1)} %get-tuple-element.29.mine_ref, ...), custom_call_target="tpu_custom_call" | custom-call | tf_op jit(solution)/shard_map/bellman_3/pallas_call | solution.py:256
  129.3 16.5 %all_to_all.53.parts_ref = f32[128,2,128]{2,1,0:T(2,128)S(1)} all-to-all(f32[128,2,128]{2,1,0:T(2,128)S(1)} %get-tuple-element.38), channel_id=1, replica_groups=mesh['y'=4,'z'=8,'x'=4,'c'=2] {'y','z','x'}, dimensions={0} | all-to-all | bytes 262144 | tf_op jit(solution)/shard_map/all_to_all | solution.py:265
  145.8 0.1 packet.1.mine_ref
  145.9 11.2 %collective-permute-start.4 = (f32[24,128]{1,0:T(8,128)S(1)}, f32[24,128]{1,0:T(8,128)S(1)}, u32[]{:S(2)}, u32[]{:S(2)}) collective-permute-start(f32[24,128]{1,0:T(8,128)S(1)} %packet.1.mine_ref), channel_id=1, source_target_pairs={{0,1},{1,0},{2,3},{3,2},{4,5},{5,4},{6,7},{7,6},{8,9},{9,8},{10,11... | collective-permute-start | bytes 36872 | tf_op jit(solution)/shard_map/ppermute | solution.py:209
  157.1 0.8 collective-permute-done.4.theirs_ref
  157.9 0.7 unpack.1
  (6 shorter events, 0.3 us)
Async XLA Ops:
  0.6 5.5 %collective-permute-start.2 = (f32[16,16,128]{2,1,0:T(8,128)}, f32[16,16,128]{2,1,0:T(8,128)S(1)}, u32[]{:S(2)}, u32[]{:S(2)}) collective-permute-start(f32[16,16,128]{2,1,0:T(8,128)} %my_costs_hbm.1), channel_id=1, source_target_pairs={{0,1},{1,0},{2,3},{3,2},{4,5},{5,4},{6,7},{7,6},{8,9},{9,8},{10,11... | collective-permute-start | bytes 393224 | tf_op jit(solution)/shard_map/ppermute | solution.py:209
  3.9 1.4 collective-permute-start
  4.0 2.1 %collective-permute-start.1 = (s32[16]{0:T(128)}, s32[16]{0:T(128)S(1)}, u32[]{:S(2)}, u32[]{:S(2)}) collective-permute-start(s32[16]{0:T(128)} %my_counts_hbm.1), channel_id=1, source_target_pairs={{0,1},{1,0},{2,3},{3,2},{4,5},{5,4},{6,7},{7,6},{8,9},{9,8},{10,11... | collective-permute-start | bytes 200 | tf_op jit(solution)/shard_map/ppermute | solution.py:209
  6.1 35.8 %collective-permute-start.3 = (f32[256,4096]{1,0:T(8,128)}, f32[256,4096]{1,0:T(8,128)S(1)}, u32[]{:S(2)}, u32[]{:S(2)}) collective-permute-start(f32[256,4096]{1,0:T(8,128)} %bitcast.5), channel_id=1, source_target_pairs={{0,1},{1,0},{2,3},{3,2},{4,5},{5,4},{6,7},{7,6},{8,9},{9,8},{10,11... | collective-permute-start | bytes 12582920 | tf_op jit(solution)/shard_map/ppermute | solution.py:209
  145.9 12.0 %collective-permute-start.4 = (f32[24,128]{1,0:T(8,128)S(1)}, f32[24,128]{1,0:T(8,128)S(1)}, u32[]{:S(2)}, u32[]{:S(2)}) collective-permute-start(f32[24,128]{1,0:T(8,128)S(1)} %packet.1.mine_ref), channel_id=1, source_target_pairs={{0,1},{1,0},{2,3},{3,2},{4,5},{5,4},{6,7},{7,6},{8,9},{9,8},{10,11... | collective-permute-start | bytes 36872 | tf_op jit(solution)/shard_map/ppermute | solution.py:209
